TPU v7x, 128 devices: a whole 4x4x4 slice. The times are simulated.
128 devices in a mesh: slab: 32 (over y, x, core), orb: 4 (over z).
Axes of the slice: x: 4, y: 4, z: 4, core: 2. Of those that a mesh axis runs over, the one named last changes fastest.
Arguments:
- orbitals: float32 [256, 64, 4096], P('orb', 'slab'), may hold values from -6 to 6
- pair_list: int32 [128, 2], P(('slab', 'orb')), may hold values from 0 to 255, as said below
- box_start: int32 [128, 3], P(('slab', 'orb')), may hold values from 0 to 63
Outputs:
- exchange_action: float32 [256, 64, 4096], P('orb', 'slab')
Inputs may be any that keep to these rules, and one draw needn't show every extreme that they name: `pair_list`: the two orbitals of a row differ.
All inputs are finite; a program needn't handle non-finite values.
Results may differ from a plain program's by a relative error of at most 0.0003.
Values sent between devices are 32-bit elements; how exact they have to be, the bound alone decides.
A program may use at most 128 MiB of HBM per device.

v0:
```python
import jax
import jax.numpy as jnp
from jax import lax
from jax.sharding import PartitionSpec as P

NX = 64
NY = 64
NZ = 64
ITERS = 16


screening = 0.02
center_eig = 6.0 + screening
half_width = 6.0
sigma_one = center_eig / half_width


def side_by_side(arrays, axis, dim, along):
    ends, at = ([], 0)
    for a in arrays[:-1]:
        at += a.shape[along]
        ends.append(at)
    both = jnp.concatenate(arrays, axis=along)
    return tuple(jnp.split(lax.all_gather(both, axis, axis=dim, tiled=True), ends, axis=along))


def operate(field):
    cells = field.shape[2]
    z_index = jnp.arange(cells, dtype=jnp.int32) % NZ
    beside = jnp.roll(field, 1, 1) + jnp.roll(field, -1, 1)
    beside = beside + jnp.roll(field, NZ, 2) + jnp.roll(field, -NZ, 2)
    upper = jnp.where(z_index == NZ - 1, jnp.roll(field, NZ - 1, 2), jnp.roll(field, -1, 2))
    lower = jnp.where(z_index == 0, jnp.roll(field, 1 - NZ, 2), jnp.roll(field, 1, 2))
    return center_eig * field - (beside + upper + lower)


def solve_screened(density):

    def sweep(step_index, state_now):
        solution, residue, update, ratio = state_now
        solution = solution + update
        residue = residue - operate(update)
        ratio_next = 1.0 / (2.0 * sigma_one - ratio)
        update = ratio_next * ratio * update + 2.0 * ratio_next / half_width * residue
        return (solution, residue, update, ratio_next)

    start_state = (
        jnp.zeros_like(density),
        density,
        density / center_eig,
        jnp.asarray(1.0 / sigma_one, jnp.float32),
    )
    return lax.fori_loop(0, ITERS, sweep, start_state)[0]


def pair_work(received):
    left = received[:, 0]
    right = received[:, 1]
    potential = solve_screened(left * right)
    return jnp.stack([-potential * right, -potential * left], axis=1)


def box_mask(starts, slab_at, slab_rows, cells):
    x_cells = slab_at * slab_rows + jnp.arange(slab_rows, dtype=jnp.int32)
    cell_index = jnp.arange(cells, dtype=jnp.int32)
    y_index = cell_index // NZ
    z_index = cell_index % NZ
    inside_x = (x_cells[None, None, :] - starts[:, :, 0:1]) % NX < NX // 2
    inside_y = (y_index[None, None, :] - starts[:, :, 1:2]) % NY < NY // 2
    inside_z = (z_index[None, None, :] - starts[:, :, 2:3]) % NZ < NZ // 2
    inside = inside_x[:, :, :, None] & (inside_y & inside_z)[:, :, None, :]
    return inside[:, None]


def body(orbitals, pair_list, box_start):
    n_slab = lax.axis_size("slab")
    n_orb = lax.axis_size("orb")
    slab_at = lax.axis_index("slab")
    orb_at = lax.axis_index("orb")
    orb_dev, slab_rows, cells = orbitals.shape
    pair_dev = pair_list.shape[0]
    devices = n_slab * n_orb
    all_pairs, all_boxes = side_by_side((pair_list, box_start), ("slab", "orb"), 0, 1)
    pair_grid = all_pairs.reshape(n_slab, n_orb, pair_dev, 2)
    box_grid = all_boxes.reshape(n_slab, n_orb, pair_dev, 3)
    row_pairs = jnp.take(pair_grid, orb_at, axis=1).transpose(1, 2, 0)
    own_y = jnp.broadcast_to(box_start[:, None, 1:2], (pair_dev, 2, 1)).reshape(-1)
    own_z = jnp.broadcast_to(box_start[:, None, 2:3], (pair_dev, 2, 1)).reshape(-1)
    boxed_frame = False
    gathered = lax.all_gather(orbitals, "orb", axis=0, tiled=True)
    starts = jnp.take(box_grid, orb_at, axis=1).transpose(1, 0, 2)
    pieces = jnp.take(gathered, row_pairs, axis=0)
    pieces = jnp.where(box_mask(starts, slab_at, slab_rows, cells), pieces, 0.0)
    outgoing = pieces.reshape(pair_dev, 2, n_slab * slab_rows, cells)
    terms = pair_work(lax.all_to_all(outgoing, "slab", split_axis=2, concat_axis=2, tiled=True))
    full_rows = n_slab * slab_rows
    spread = jnp.broadcast_to(
        terms.reshape(pair_dev, 2, n_slab, 1, slab_rows, cells),
        (pair_dev, 2, n_slab, n_orb, slab_rows, cells),
    )
    spread = spread.reshape(pair_dev, 2, devices * slab_rows, cells)
    returned = lax.all_to_all(spread, ("slab", "orb"), split_axis=2, concat_axis=2, tiled=True)
    owners = (
        all_pairs.reshape(devices, pair_dev, 2).transpose(1, 2, 0).reshape(-1) - orb_at * orb_dev
    )
    one_hot = (jnp.arange(orb_dev, dtype=jnp.int32)[:, None] == owners[None, :]).astype(jnp.float32)
    action = jnp.dot(
        one_hot,
        returned.reshape(pair_dev * 2 * devices, slab_rows * cells),
        precision=lax.Precision.HIGHEST,
        preferred_element_type=jnp.float32,
    )
    return action.reshape(orb_dev, slab_rows, cells)


def solution(mesh):
    return jax.shard_map(
        body,
        mesh=mesh,
        in_specs=(P("orb", "slab", None), P(("slab", "orb"), None), P(("slab", "orb"), None)),
        out_specs=P("orb", "slab", None),
        check_vma=False,
    )
```

profile of v0, /device:TPU:1, one launch (start us, length us, event | category | flops | bytes accessed | tf_op | source)
XLA Modules:
  0.0 380.7 jit_solution(14061761828574327259)
XLA Ops:
  6.5 0.7 all-gather.3.cloned.1.call-update
  7.4 50.4 %all-gather = s32[128,1,5]{2,1,0:T(1,128)S(1)} all-gather(s32[1,1,5]{2,1,0:T(1,128)S(1)} %add_bitcast_fusion), channel_id=1, replica_groups=mesh['slab'=32,'orb'=4] {'slab','orb'}, dimensions={0}, use_global_device_ids=true | all-gather | bytes 2580 | tf_op jit(solution)/shard_map/all_gather | solution.py:24
  58.7 0.6 fusion.19
  59.3 0.6 and.127
  59.9 0.7 and.128
  60.8 35.6 %all-gather.3.cloned.1.call-done = f32[256,2,4096]{2,1,0:T(2,128)} async-done(((f32[64,2,4096]{2,1,0:T(2,128)}), f32[256,2,4096]{2,1,0:T(2,128)}) %all-gather.3.cloned.1.call-update) | async-done | bytes 8388624 | tf_op jit(solution)/shard_map/all_gather | solution.py:90
  96.4 6.2 %gather_fusion = f32[64,2,4096]{2,1,0:T(2,128)S(1)} fusion(f32[256,2,4096]{2,1,0:T(2,128)} %all-gather.3.cloned.1.call-done, s32[1024]{0:T(1024)S(1)} %pad_clamp_fusion), kind=kCustom, calls=%fused_computation | custom fusion | bytes 4194560 | tf_op jit(solution)/shard_map/jit(_take)/gather | solution.py:92
  102.6 2.4 gather.17
  105.0 5.6 %fusion.11 = f32[1,2,64,4096]{3,1,0,2:T(2,128)} fusion(f32[1,2,64,4096]{3,2,1,0:T(8,128)} %gather.17, pred[2,64]{0,1:T(8,128)(4,1)S(1)} %copy.15, pred[64,4096]{1,0:T(8,128)(4,1)S(1)} %broadcast_and_fusion), kind=kLoop, calls=%fused_computation.22 | loop fusion | flops 1048576 | bytes 4456576 | tf_op jit(solution)/shard_map/jit(_where)/select_n | solution.py:93
  110.6 7.7 %all-to-all-start = ((f32[1,2,64,4096]{3,1,0,2:T(2,128)}), f32[1,2,64,4096]{3,1,0,2:T(2,128)S(1)}, u32[]{:S(2)}, u32[]{:S(2)}) async-start(f32[1,2,64,4096]{3,1,0,2:T(2,128)} %fusion.11), calls=%async_computation | async-start | bytes 4194304 | tf_op jit(solution)/shard_map/all_to_all | solution.py:95
  118.4 28.5 %all-to-all-done = f32[1,2,64,4096]{3,1,0,2:T(2,128)S(1)} async-done(((f32[1,2,64,4096]{3,1,0,2:T(2,128)}), f32[1,2,64,4096]{3,1,0,2:T(2,128)S(1)}, u32[]{:S(2)}, u32[]{:S(2)}) %all-to-all-start) | async-done | bytes 2097184 | tf_op jit(solution)/shard_map/all_to_all | solution.py:95
  146.9 2.3 broadcast_multiply_fusion
  149.2 0.6 copy.19
  149.9 0.6 copy.18
  150.5 54.3 %while.19 = (s32[]{:T(128)}, f32[1,64,4096]{2,1,0:T(8,128)S(1)}, f32[1,64,4096]{2,1,0:T(8,128)S(1)}, f32[1,64,4096]{2,1,0:T(8,128)S(1)}, f32[]{:T(128)}, /*index...) while((s32[]{:T(128)}, f32[1,64,4096]{2,1,0:T(8,128)S(1)}, ...), condition=%wide.region_1.2_spmd.clone, body=%wide.region_0.1_spmd.clone.sunk | while | flops 6062087 | bytes 32522416 | solution.py:53
  151.5 0.4 fusion.57
  152.4 1.5 multiply_add_fusion.2
  155.2 0.4 fusion.54
  155.8 1.5 multiply_add_fusion.2
  159.2 1.5 multiply_add_fusion.2
  162.0 0.4 fusion.54
  162.6 1.5 multiply_add_fusion.2
  166.0 1.5 multiply_add_fusion.2
  168.8 0.4 fusion.54
  169.3 1.5 multiply_add_fusion.2
  172.7 1.5 multiply_add_fusion.2
  175.6 0.4 fusion.54
  176.1 1.5 multiply_add_fusion.2
  179.5 1.5 multiply_add_fusion.2
  182.0 0.4 fusion.57
  182.9 1.5 multiply_add_fusion.2
  186.3 1.5 multiply_add_fusion.2
  189.7 1.5 multiply_add_fusion.2
  193.1 1.5 multiply_add_fusion.2
  196.5 1.5 multiply_add_fusion.2
  199.9 1.5 multiply_add_fusion.2
  203.3 1.5 multiply_add_fusion.2
  204.8 5.3 %fusion.14 = (f32[1,64,4096]{2,0,1:T(1,128)S(1)}, f32[1,64,4096]{2,0,1:T(1,128)S(1)}) fusion(f32[1,2,64,4096]{3,1,0,2:T(2,128)} %copy-done, f32[1,64,4096]{2,1,0:T(8,128)S(1)} %get-tuple-element.32), kind=kLoop, calls=%fused_computation.38 | loop fusion | flops 786432 | bytes 5242880 | tf_op jit(solution)/shard_map/mul | solution.py:60
  210.1 4.0 %pad_maximum_fusion = f32[1,2,32,1,2,4096]{5,0,4,3,2,1:T(1,128)S(1)} fusion(f32[1,1,32,1,2,4096]{5,0,4,3,2,1:T(1,128)S(1)} %bitcast.60, f32[1,1,32,1,2,4096]{5,0,4,3,2,1:T(1,128)S(1)} %bitcast.59), kind=kLoop, calls=%fused_computation.19 | loop fusion | flops 524288 | bytes 4194304 | tf_op jit(solution)/shard_map/stack | solution.py:60
  214.1 1.9 copy.38
  216.0 7.5 %broadcast_in_dim.91 = f32[2,32,4,2,4096]{4,0,3,2,1:T(2,128)} broadcast(f32[2,32,2,4096]{3,0,2,1:T(2,128)S(1)} %bitcast.58), dimensions={0,1,3,4} | broadcast | bytes 10485760 | tf_op jit(solution)/shard_map/broadcast_in_dim | solution.py:97
  223.5 6.4 %all-to-all-start.1 = ((f32[1,2,256,4096]{3,1,0,2:T(2,128)}), f32[1,2,256,4096]{3,1,0,2:T(2,128)}, u32[]{:S(2)}, u32[]{:S(2)}) async-start(f32[1,2,256,4096]{3,1,0,2:T(2,128)} %bitcast.55), calls=%async_computation.1 | async-start | bytes 16777216 | tf_op jit(solution)/shard_map/all_to_all | solution.py:102
  230.0 102.7 %all-to-all-done.1 = f32[1,2,256,4096]{3,1,0,2:T(2,128)} async-done(((f32[1,2,256,4096]{3,1,0,2:T(2,128)}), f32[1,2,256,4096]{3,1,0,2:T(2,128)}, u32[]{:S(2)}, u32[]{:S(2)}) %all-to-all-start.1) | async-done | bytes 8388640 | tf_op jit(solution)/shard_map/all_to_all | solution.py:102
  332.7 11.5 %copy.22 = f32[1,2,256,4096]{3,2,1,0:T(8,128)} copy(f32[1,2,256,4096]{3,1,0,2:T(2,128)} %all-to-all-done.1) | data formatting | bytes 16777216 | tf_op jit(solution)/shard_map/all_to_all | solution.py:102
  344.2 10.0 %reshape.587 = f32[256,8192]{1,0:T(8,128)} reshape(f32[1,2,256,4096]{3,2,1,0:T(8,128)} %copy.22) | data formatting | bytes 16777216 | tf_op jit(solution)/shard_map/reshape | solution.py:109
  354.2 9.0 %copy.23 = f32[8192,256]{1,0:T(8,128)} copy(f32[8192,256]{0,1:T(8,128)} %bitcast.57) | data formatting | bytes 16777216 | tf_op jit(solution)/shard_map/dot_general | solution.py:107
  363.2 7.7 %fusion.21 = f32[64,2,4096]{2,0,1:T(8,128)S(1)} fusion(f32[2,4096,256]{2,1,0:T(8,128)} %bitcast.56, s32[256]{0:T(256)S(1)} %bitcast.65), kind=kOutput, calls=%fused_computation.49 | convolution fusion | flops 1610629120 | bytes 10486784 | tf_op jit(solution)/shard_map/dot_general | solution.py:107
  370.9 2.9 copy.24
  (184 shorter events, 28.1 us)
Async XLA Ops:
  6.5 0.7 copy-start.1
  6.5 0.7 copy-start.2
  6.5 89.9 %all-gather.3.cloned.1.call-start = ((), (), s32[]{:S(2)}) async-start(), calls=%async_computation.2 | async-start | bytes 10485760 | tf_op jit(solution)/shard_map/all_gather | solution.py:90
  110.6 36.2 %all-to-all-start = ((f32[1,2,64,4096]{3,1,0,2:T(2,128)}), f32[1,2,64,4096]{3,1,0,2:T(2,128)S(1)}, u32[]{:S(2)}, u32[]{:S(2)}) async-start(f32[1,2,64,4096]{3,1,0,2:T(2,128)} %fusion.11), calls=%async_computation | async-start | bytes 4194304 | tf_op jit(solution)/shard_map/all_to_all | solution.py:95
  146.9 2.3 copy-start
  223.5 109.2 %all-to-all-start.1 = ((f32[1,2,256,4096]{3,1,0,2:T(2,128)}), f32[1,2,256,4096]{3,1,0,2:T(2,128)}, u32[]{:S(2)}, u32[]{:S(2)}) async-start(f32[1,2,256,4096]{3,1,0,2:T(2,128)} %bitcast.55), calls=%async_computation.1 | async-start | bytes 16777216 | tf_op jit(solution)/shard_map/all_to_all | solution.py:102
Sparse Core Ops, SparseCore 0:
  9.0 87.3 all-gather.2
where the time goes:
time: 382 us; the launch traced here: 381 us
  waiting for transfers between devices  168 us (44%)
  local copies, waits for them, and re-layouts  78.2 us (20%)
  blocking collectives  50.4 us (13%)
  other arithmetic  47.3 us (12%)
  starting transfers between devices  14.1 us (4%)
  between operations  13.6 us (4%)
  matrix products  7.74 us (2%)
    all_to_all x1, waiting for transfers between devices, body(): lax.all_to_all(spread, ('slab', 'orb'), split_axis=2, concat_axis=2, tile...  103 us
    all_gather x1, blocking collectives, side_by_side(): lax.all_gather(both, axis, axis=dim, tiled=True)  50.4 us
    all_gather x1, waiting for transfers between devices, body(): gathered = lax.all_gather(orbitals, 'orb', axis=0, tiled=True)  35.6 us
    all_to_all x1, waiting for transfers between devices, body(): lax.all_to_all(outgoing, 'slab', split_axis=2, concat_axis=2, tiled=True)  28.5 us
    add x16, other arithmetic, sweep(): ratio_next * ratio * update + 2.0 * ratio_next / half_width * residue  23.7 us
    dot_general x2, local copies, waits for them, and re-layouts, body(): jnp.dot(one_hot, returned.reshape(pair_dev * 2 * devices, slab_rows * cel...  11.9 us
    all_to_all x1, local copies, waits for them, and re-layouts, body(): lax.all_to_all(spread, ('slab', 'orb'), split_axis=2, concat_axis=2, tile...  11.5 us
    reshape x1, local copies, waits for them, and re-layouts, body(): returned.reshape(pair_dev * 2 * devices, slab_rows * cells)  9.99 us
  transfers between devices with their start and end apart: 3, of which 3 were waited for; matrix products, arithmetic and copies ran while one was open for 1% of the time, Pallas kernels for 0%

commit v1 on v0

v1 whole, which is shorter than its diff:
```python
import functools

import jax
import jax.numpy as jnp
import numpy as np
from jax import lax
from jax.experimental import pallas as pl
from jax.experimental.pallas import tpu as pltpu
from jax.sharding import PartitionSpec as P

ITERS = 16
SCREENING = 0.02
CENTER_EIG = 6.0 + SCREENING
HALF_WIDTH = 6.0

MESH = pl.DeviceIdType.MESH
VMEM = pl.BlockSpec(memory_space=pltpu.VMEM)
SMEM = pl.BlockSpec(memory_space=pltpu.SMEM)
F32 = jnp.float32
I32 = jnp.int32
META = 8


def chebyshev_weights():
    cheb = np.polynomial.chebyshev
    theta, delta = CENTER_EIG, HALF_WIDTH
    sigma = theta / delta
    potential, residue, update = np.zeros(1), np.ones(1), np.ones(1) / theta
    ratio = 1.0 / sigma
    for _ in range(ITERS):
        potential = cheb.chebadd(potential, update)
        applied = cheb.chebsub(theta * update, 6.0 * cheb.chebmulx(update))
        residue = cheb.chebsub(residue, applied)
        ratio_next = 1.0 / (2.0 * sigma - ratio)
        update = cheb.chebadd(ratio_next * ratio * update, 2.0 * ratio_next / delta * residue)
        ratio = ratio_next
    return [float(c) for c in potential[:ITERS]]


WEIGHTS = chebyshev_weights()


def greet(n_slab, n_orb):
    s, o = lax.axis_index("slab"), lax.axis_index("orb")
    barrier = pltpu.get_barrier_semaphore()
    for d in range(1, n_orb):
        pl.semaphore_signal(barrier, 1, device_id={"orb": lax.rem(o + d, n_orb)}, device_id_type=MESH)

    def signal(d, _):
        pl.semaphore_signal(barrier, 1, device_id={"slab": lax.rem(s + d, n_slab)}, device_id_type=MESH)
        return 0

    lax.fori_loop(1, n_slab, signal, 0)
    pl.semaphore_wait(barrier, n_orb - 1 + n_slab - 1)


def remote(src, dst, send, recv, device):
    return pltpu.make_async_remote_copy(
        src_ref=src, dst_ref=dst, send_sem=send, recv_sem=recv, device_id=device, device_id_type=MESH
    )


def share_kernel(n_slab, n_orb, row_ref, out_ref, own_sem, send_o, recv_o, send_s, recv_s):
    s, o = lax.axis_index("slab"), lax.axis_index("orb")
    own = pltpu.make_async_copy(row_ref, out_ref.at[s, o], own_sem)
    own.start()
    greet(n_slab, n_orb)
    copies = [
        remote(row_ref, out_ref.at[s, o], send_o.at[d - 1], recv_o.at[d - 1], {"orb": lax.rem(o + d, n_orb)})
        for d in range(1, n_orb)
    ]
    for copy in copies:
        copy.start()
    own.wait()
    for copy in copies:
        copy.wait()

    def to(d):
        return remote(
            out_ref.at[s], out_ref.at[s], send_s.at[d - 1], recv_s.at[d - 1], {"slab": lax.rem(s + d, n_slab)}
        )

    def start(d, _):
        to(d).start()
        return 0

    def wait(d, _):
        to(d).wait()
        return 0

    lax.fori_loop(1, n_slab, start, 0)
    lax.fori_loop(1, n_slab, wait, 0)


def lanes_and_rows():
    lane = lax.broadcasted_iota(I32, (8, 128), 1)
    row = lax.broadcasted_iota(I32, (8, 128), 0)
    return lane, row


def inside_y(j, by, lane, row):
    y = 8 * j + 2 * (row >> 1) + (lane >> 6)
    return ((y - by) & 63) < 32


def pack_kernel(n_pairs, n_orb, orb_dev, meta_ref, orb_ref, out_ref):
    o = lax.axis_index("orb")
    lane, row = lanes_and_rows()
    zz = lane & 63

    def one(p, _):
        i, j = meta_ref[META * p], meta_ref[META * p + 1]
        by, bz = meta_ref[META * p + 3], meta_ref[META * p + 4]
        hold_i, hold_j = lax.div(i, orb_dev) == o, lax.div(j, orb_dev) == o
        li, lj = lax.rem(i, orb_dev), lax.rem(j, orb_dev)
        whole = []
        for k in range(8):
            a = jnp.where(hold_i, orb_ref[li, 8 * k : 8 * k + 8, :], 1.0)
            b = jnp.where(hold_j, orb_ref[lj, 8 * k : 8 * k + 8, :], 1.0)
            whole.append(a * b)
        folded = []
        for k in range(4):
            v = jnp.where(inside_y(k, by, lane, row), whole[k], whole[k + 4])
            b = bz if k < 2 else (bz + 32) & 63
            v = jnp.where(
                zz + b < 64, pltpu.roll(v, (128 - b) & 127, 1), pltpu.roll(v, (64 - b) & 127, 1)
            )
            folded.append(v)
        for k in range(2):
            out_ref[lax.rem(p, n_orb), lax.div(p, n_orb), 8 * k : 8 * k + 8, :] = jnp.where(
                zz < 32, folded[k], folded[k + 2]
            )
        return 0

    lax.fori_loop(0, n_pairs, one, 0)


def gather_kernel(
    n_slab, n_orb, orb_dev, meta_ref, packed_ref, held_ref, box_ref,
    density, own_sem, send_o, recv_o, send_s, recv_s,
):
    s, o = lax.axis_index("slab"), lax.axis_index("orb")
    own = pltpu.make_async_copy(packed_ref.at[o], held_ref.at[o], own_sem)
    own.start()
    greet(n_slab, n_orb)
    copies = []
    for d in range(1, n_orb):
        to = lax.rem(o + d, n_orb)
        copies.append(remote(packed_ref.at[to], held_ref.at[o], send_o.at[d - 1], recv_o.at[d - 1], {"orb": to}))
    for copy in copies:
        copy.start()
    own.wait()
    for copy in copies:
        copy.wait()

    def form(q, _):
        p = q * n_orb + o
        oi, oj = lax.div(meta_ref[META * p], orb_dev), lax.div(meta_ref[META * p + 1], orb_dev)
        left = held_ref[oi, q]
        right = held_ref[oj, q]
        density[q] = jnp.where(oi == oj, left, left * right)
        return 0

    lax.fori_loop(0, n_slab, form, 0)
    mine = pltpu.make_async_copy(density.at[s], box_ref.at[s], own_sem)
    mine.start()

    def to(d):
        slab = lax.rem(s + d, n_slab)
        return remote(density.at[slab], box_ref.at[s], send_s.at[d - 1], recv_s.at[d - 1], {"slab": slab})

    def start(d, _):
        to(d).start()
        return 0

    def wait(d, _):
        to(d).wait()
        return 0

    lax.fori_loop(1, n_slab, start, 0)
    mine.wait()
    lax.fori_loop(1, n_slab, wait, 0)


def solve_kernel(start_ref, weight_ref, box_ref, out_ref, rows_a, rows_b, source, ping, pong):
    bx, by, bz = start_ref[0, 0], start_ref[0, 1], start_ref[0, 2]
    by32 = by & 31
    lane, row = lanes_and_rows()
    zz = lane & 63
    in_z = (zz >= 16) & (zz < 48)

    def place(xm, _):
        x0, x1 = (bx + xm - 8) & 63, (bx + xm + 16) & 63
        v0 = box_ref[x0 >> 1, pl.ds(x0 & 1, 8, 2), :]
        v1 = box_ref[x1 >> 1, pl.ds(x1 & 1, 8, 2), :]
        v0 = jnp.where(xm >= 8, v0, 0.0)
        v1 = jnp.where(xm < 16, v1, 0.0)
        for h in range(2):
            for q in range(2):
                a = pltpu.roll(v0, (16 - 64 * h - 32 * q) % 128, 1)
                b = pltpu.roll(v1, (80 - 64 * h - 32 * q) % 128, 1)
                v = jnp.where(in_z, jnp.where(lane < 64, a, b), 0.0)
                for dup in range(4):
                    rows_a[xm, pl.ds(32 * dup + 16 * q + h, 8, 2), :] = v
        for k in range(6):
            u = 6 * row + k - 8
            v = rows_a[xm, pl.ds(by32 + 24 + k, 8, 6), :]
            source[xm, k] = jnp.where((u >= 0) & (u < 32), v, 0.0)
        return 0

    lax.fori_loop(0, 24, place, 0)

    def close(ref):
        for k in range(6):
            ref[0, k] = pltpu.roll(ref[24, k], 64, 1)
            ref[25, k] = pltpu.roll(ref[1, k], 64, 1)

    def neighbours(ref, x):
        at = [ref[x, k] for k in range(6)]
        sums = []
        for k in range(6):
            below = at[k - 1] if k > 0 else pltpu.roll(at[5], 1, 0)
            above = at[k + 1] if k < 5 else pltpu.roll(at[0], 7, 0)
            sums.append(
                (ref[x - 1, k] + ref[x + 1, k])
                + (below + above)
                + (pltpu.roll(at[k], 1, 1) + pltpu.roll(at[k], 127, 1))
            )
        return sums

    first = weight_ref[ITERS - 1]
    for xm in range(24):
        for k in range(6):
            ping[xm + 1, k] = first * source[xm, k]
            pong[xm + 1, k] = jnp.zeros((8, 128), F32)
    close(ping)

    def step(now, older, index):
        weight = weight_ref[index]
        for xm in range(24):
            sums = neighbours(now, xm + 1)
            for k in range(6):
                older[xm + 1, k] = weight * source[xm, k] + (sums[k] * (1.0 / 3.0) - older[xm + 1, k])
        close(older)

    def two(n, _):
        step(ping, pong, ITERS - 2 - 2 * n)
        step(pong, ping, ITERS - 3 - 2 * n)
        return 0

    lax.fori_loop(0, (ITERS - 2) // 2, two, 0)
    weight = weight_ref[0]
    for xm in range(24):
        sums = neighbours(ping, xm + 1)
        for k in range(6):
            rows_b[xm, pl.ds(k, 8, 6), :] = weight * source[xm, k] + (
                sums[k] * (1.0 / 6.0) - pong[xm + 1, k]
            )

    def dup_rows(xm, _):
        for m in range(4):
            v = rows_b[xm, 8 + 8 * m : 16 + 8 * m, :]
            rows_a[xm, 8 * m : 8 * m + 8, :] = v
            rows_a[xm, 32 + 8 * m : 40 + 8 * m, :] = v
        return 0

    lax.fori_loop(0, 24, dup_rows, 0)

    def give(ux, _):
        x = (bx + ux) & 31
        half = (ux >= 16).astype(I32)
        xm = ux + 8 - 24 * half
        pieces = []
        for h in range(2):
            for q in range(2):
                v = rows_a[xm, pl.ds(32 - by32 + 16 * q + h, 8, 2), :]
                pieces.append(pltpu.roll(v, (64 * h + 32 * q - 16 + 128 - 64 * half) & 127, 1))
        v = jnp.where(
            lane < 64,
            jnp.where(zz < 32, pieces[0], pieces[1]),
            jnp.where(zz < 32, pieces[2], pieces[3]),
        )
        out_ref[x >> 1, pl.ds(x & 1, 8, 2), :] = v
        return 0

    lax.fori_loop(0, 32, give, 0)


def scatter_kernel(
    n_slab, n_orb, orb_dev, meta_ref, potential_ref, held_ref, out_ref,
    mine, terms, own_sem, send_o, recv_o, send_s, recv_s,
):
    s, o = lax.axis_index("slab"), lax.axis_index("orb")
    half = n_slab // 2
    own = pltpu.make_async_copy(potential_ref.at[lax.rem(s, half)], mine.at[s], own_sem)
    own.start()
    greet(n_slab, n_orb)

    def to(d):
        slab = lax.rem(s + d, n_slab)
        return remote(
            potential_ref.at[lax.rem(slab, half)], mine.at[s], send_s.at[d - 1], recv_s.at[d - 1], {"slab": slab}
        )

    def start(d, _):
        to(d).start()
        return 0

    def wait(d, _):
        to(d).wait()
        return 0

    lax.fori_loop(1, n_slab, start, 0)
    own.wait()
    lax.fori_loop(1, n_slab, wait, 0)

    def form(q, _):
        p = q * n_orb + o
        oi, oj = lax.div(meta_ref[META * p], orb_dev), lax.div(meta_ref[META * p + 1], orb_dev)
        value = mine[q]
        left = held_ref[oi, q]
        right = held_ref[oj, q]
        for dest in range(n_orb):
            factor = jnp.where(oi == oj, 1.0, jnp.where(oi == dest, -right, -left))
            terms[dest, q] = value * factor
        return 0

    lax.fori_loop(0, n_slab, form, 0)
    keep = pltpu.make_async_copy(terms.at[o], out_ref.at[o], own_sem)
    keep.start()
    copies = []
    for d in range(1, n_orb):
        dest = lax.rem(o + d, n_orb)
        copies.append(remote(terms.at[dest], out_ref.at[o], send_o.at[d - 1], recv_o.at[d - 1], {"orb": dest}))
    for copy in copies:
        copy.start()
    keep.wait()
    for copy in copies:
        copy.wait()


def add_kernel(n_pairs, n_orb, orb_dev, meta_ref, terms_ref, orb_ref, out_ref):
    s, o = lax.axis_index("slab"), lax.axis_index("orb")
    lane, row = lanes_and_rows()
    z = lane & 63
    x = 2 * s + (row & 1)

    def clear(n, _):
        out_ref[n] = jnp.zeros(out_ref.shape[1:], F32)
        return 0

    lax.fori_loop(0, orb_dev, clear, 0)

    def one(p, _):
        i, j = meta_ref[META * p], meta_ref[META * p + 1]
        bx, by, bz = meta_ref[META * p + 2], meta_ref[META * p + 3], meta_ref[META * p + 4]
        hold_i, hold_j = lax.div(i, orb_dev) == o, lax.div(j, orb_dev) == o
        li, lj = lax.rem(i, orb_dev), lax.rem(j, orb_dev)

        def unfolded():
            in_xz = (((x - bx) & 63) < 32) & (((z - bz) & 63) < 32)
            wide = []
            for k in range(4):
                v = terms_ref[lax.rem(p, n_orb), lax.div(p, n_orb), 8 * (k % 2) : 8 * (k % 2) + 8, :]
                b = bz if k < 2 else (bz + 32) & 63
                v = jnp.where(z >= b, pltpu.roll(v, b, 1), pltpu.roll(v, (b + 64) & 127, 1))
                wide.append(jnp.where(in_xz, v, 0.0))
            keep = [inside_y(k, by, lane, row) for k in range(4)]
            return [jnp.where(keep[k], wide[k], 0.0) for k in range(4)] + [
                jnp.where(keep[k], 0.0, wide[k]) for k in range(4)
            ]

        both = hold_i & hold_j

        @pl.when(both)
        def _():
            values = unfolded()
            for k in range(8):
                rows = slice(8 * k, 8 * k + 8)
                out_ref[li, rows, :] = out_ref[li, rows, :] - values[k] * orb_ref[lj, rows, :]
                out_ref[lj, rows, :] = out_ref[lj, rows, :] - values[k] * orb_ref[li, rows, :]

        @pl.when((hold_i | hold_j) & jnp.logical_not(both))
        def _():
            at = jnp.where(hold_i, li, lj)
            values = unfolded()
            for k in range(8):
                rows = slice(8 * k, 8 * k + 8)
                out_ref[at, rows, :] = out_ref[at, rows, :] + values[k]

        return 0

    lax.fori_loop(0, n_pairs, one, 0)


def peer_sems(n_slab, n_orb):
    return [
        pltpu.SemaphoreType.DMA,
        pltpu.SemaphoreType.DMA((n_orb - 1,)),
        pltpu.SemaphoreType.DMA((n_orb - 1,)),
        pltpu.SemaphoreType.DMA((n_slab - 1,)),
        pltpu.SemaphoreType.DMA((n_slab - 1,)),
    ]


def remote_params(identity):
    return pltpu.CompilerParams(collective_id=identity, has_side_effects=True, vmem_limit_bytes=40 << 20)


def body(orbitals, pair_list, box_start):
    n_slab, n_orb = lax.axis_size("slab"), lax.axis_size("orb")
    orb_dev, planes, cells = orbitals.shape
    n_pairs = n_slab * n_orb
    slot = (16, 128)
    rows = orbitals.reshape(orb_dev, planes, cells // 128, 128).transpose(0, 2, 1, 3)
    rows = rows.reshape(orb_dev, planes * cells // 128, 128)
    own = jnp.pad(jnp.concatenate([pair_list, box_start], axis=1), ((0, 0), (0, 123)))
    meta = pl.pallas_call(
        functools.partial(share_kernel, n_slab, n_orb),
        out_shape=jax.ShapeDtypeStruct((n_slab, n_orb, 1, 128), I32),
        in_specs=[VMEM],
        out_specs=VMEM,
        scratch_shapes=peer_sems(n_slab, n_orb),
        compiler_params=remote_params(0),
        name="share",
    )(own)
    meta = meta.reshape(n_pairs, 128)[:, :META].reshape(-1)
    packed = pl.pallas_call(
        functools.partial(pack_kernel, n_pairs, n_orb, orb_dev),
        out_shape=jax.ShapeDtypeStruct((n_orb, n_slab) + slot, F32),
        in_specs=[SMEM, VMEM],
        out_specs=VMEM,
        name="pack",
    )(meta, rows)
    held, box = pl.pallas_call(
        functools.partial(gather_kernel, n_slab, n_orb, orb_dev),
        out_shape=[
            jax.ShapeDtypeStruct((n_orb, n_slab) + slot, F32),
            jax.ShapeDtypeStruct((n_slab,) + slot, F32),
        ],
        in_specs=[SMEM, VMEM],
        out_specs=[VMEM, VMEM],
        scratch_shapes=[pltpu.VMEM((n_slab,) + slot, F32)] + peer_sems(n_slab, n_orb),
        compiler_params=remote_params(1),
        name="gather",
    )(meta, packed)
    weights = jnp.asarray(np.asarray(WEIGHTS, np.float32))
    potential = pl.pallas_call(
        solve_kernel,
        out_shape=jax.ShapeDtypeStruct((n_slab // 2,) + slot, F32),
        in_specs=[SMEM, SMEM, VMEM],
        out_specs=VMEM,
        scratch_shapes=[
            pltpu.VMEM((24, 128, 128), F32),
            pltpu.VMEM((24, 48, 128), F32),
            pltpu.VMEM((24, 6, 8, 128), F32),
            pltpu.VMEM((26, 6, 8, 128), F32),
            pltpu.VMEM((26, 6, 8, 128), F32),
        ],
        name="solve",
    )(box_start, weights, box)
    terms = pl.pallas_call(
        functools.partial(scatter_kernel, n_slab, n_orb, orb_dev),
        out_shape=jax.ShapeDtypeStruct((n_orb, n_slab) + slot, F32),
        in_specs=[SMEM, VMEM, VMEM],
        out_specs=VMEM,
        scratch_shapes=[
            pltpu.VMEM((n_slab,) + slot, F32),
            pltpu.VMEM((n_orb, n_slab) + slot, F32),
        ]
        + peer_sems(n_slab, n_orb),
        compiler_params=remote_params(2),
        name="scatter",
    )(meta, potential, held)
    action = pl.pallas_call(
        functools.partial(add_kernel, n_pairs, n_orb, orb_dev),
        out_shape=jax.ShapeDtypeStruct(rows.shape, F32),
        in_specs=[SMEM, VMEM, VMEM],
        out_specs=VMEM,
        name="add",
    )(meta, terms, rows)
    action = action.reshape(orb_dev, cells // 128, planes, 128).transpose(0, 2, 1, 3)
    return action.reshape(orb_dev, planes, cells)


def solution(mesh):
    return jax.shard_map(
        body,
        mesh=mesh,
        in_specs=(P("orb", "slab", None), P(("slab", "orb"), None), P(("slab", "orb"), None)),
        out_specs=P("orb", "slab", None),
        check_vma=False,
    )
```

time: 382 us -> 107 us (0.28)
  waiting for transfers between devices: 168 us -> 0 us
  Pallas kernels: 0 us -> 102 us
  local copies, waits for them, and re-layouts: 78.2 us -> 4.48 us
  blocking collectives: 50.4 us -> 0 us
  other arithmetic: 47.3 us -> 0.75 us
  starting transfers between devices: 14.1 us -> 0 us
  between operations: 13.6 us -> 0.05 us
  matrix products: 7.74 us -> 0 us
    all_to_all x2 -> x0, waiting for transfers between devices: 131 us -> none  [the longest x1 103 us: body(): lax.all_to_all(spread, ('slab', 'orb'), split_axis=2, concat_axis=2, tile...]
    pallas_call x0 -> x6, Pallas kernels: none -> 102 us  [the longest x1 25.1 us: body(): pl.pallas_call(functools.partial(scatter_kernel, n_slab, n_orb, orb_dev),...]
    all_gather x1 -> x0, blocking collectives: 50.4 us -> none  [side_by_side(): lax.all_gather(both, axis, axis=dim, tiled=True)]
    all_gather x1 -> x0, waiting for transfers between devices: 35.6 us -> none  [body(): gathered = lax.all_gather(orbitals, 'orb', axis=0, tiled=True)]
    add x33 -> x0, other arithmetic: 29 us -> none  [the longest x16 23.7 us: sweep(): ratio_next * ratio * update + 2.0 * ratio_next / half_width * residue]
    slice x128 -> x0, local copies, waits for them, and re-layouts: 23.5 us -> none  [the longest x32 6.82 us: operate(): jnp.roll(field, -1, 2)]
    all_to_all x2 -> x0, starting transfers between devices: 14.1 us -> none  [the longest x1 7.71 us: body(): lax.all_to_all(outgoing, 'slab', split_axis=2, concat_axis=2, tiled=True)]
    dot_general x2 -> x0, local copies, waits for them, and re-layouts: 11.9 us -> none  [body(): jnp.dot(one_hot, returned.reshape(pair_dev * 2 * devices, slab_rows * cel...]
  transfers between devices with their start and end apart: 3 -> 0, of which waited for: 3 -> 0; matrix products, arithmetic and copies ran while one was open for 1% -> 0% of each run, Pallas kernels for 0% -> 0%
where the time goes in v1:
time: 107 us
  Pallas kernels  102 us (95%)
  local copies, waits for them, and re-layouts  4.48 us (4%)
    pallas_call x1, Pallas kernels, body(): pl.pallas_call(functools.partial(scatter_kernel, n_slab, n_orb, orb_dev),...  25.1 us
    pallas_call x1, Pallas kernels, body(): pl.pallas_call(functools.partial(gather_kernel, n_slab, n_orb, orb_dev),...  24.2 us
    pallas_call x1, Pallas kernels, body(): pl.pallas_call(functools.partial(share_kernel, n_slab, n_orb), out_shape=...  17.1 us
    pallas_call x1, Pallas kernels, body(): pl.pallas_call(functools.partial(pack_kernel, n_pairs, n_orb, orb_dev), o...  13.7 us
    pallas_call x1, Pallas kernels, body(): pl.pallas_call(solve_kernel, out_shape=jax.ShapeDtypeStruct((n_slab // 2,...  12.1 us
    pallas_call x1, Pallas kernels, body(): pl.pallas_call(functools.partial(add_kernel, n_pairs, n_orb, orb_dev), ou...  9.89 us
    unnamed x10, local copies, waits for them, and re-layouts  3.8 us

profile of v1, /device:TPU:1, one launch (start us, length us, event | category | flops | bytes accessed | tf_op | source)
XLA Modules:
  0.0 107.4 jit_solution(17850620694905392250)
XLA Ops:
  0.0 0.7 pad_add_fusion
  0.8 17.1 %share.1 = s32[32,4,1,128]{3,2,1,0:T(1,128)S(1)} custom-call(s32[1,128]{1,0:T(1,128)S(1)} %pad.4.row_ref), custom_call_target="tpu_custom_call" | custom-call | tf_op jit(solution)/shard_map/share/pallas_call | solution.py:418
  17.8 0.7 reshape.19.meta_ref
  18.5 0.0 copy-start.4
  18.5 13.7 %pack.1.packed_ref = f32[4,32,16,128]{3,2,1,0:T(8,128)} custom-call(s32[1024]{0:T(1024)} %reshape.19.meta_ref, f32[64,64,128]{2,1,0:T(8,128)} %bitcast.13), custom_call_target="tpu_custom_call" | custom-call | tf_op jit(solution)/shard_map/pack/pallas_call | solution.py:428
  32.2 0.0 copy-done.4
  32.2 0.0 copy-start
  32.2 1.2 %copy-done = f32[4,32,16,128]{3,2,1,0:T(8,128)S(1)} copy-done((f32[4,32,16,128]{3,2,1,0:T(8,128)S(1)}, f32[4,32,16,128]{3,2,1,0:T(8,128)}, u32[]{:S(2)}) %copy-start) | copy-done | bytes 1048600
  33.5 24.2 %gather.1 = (f32[4,32,16,128]{3,2,1,0:T(8,128)S(1)}, f32[32,16,128]{2,1,0:T(8,128)S(1)}) custom-call(s32[1024]{0:T(1024)S(1)} %copy-done.4, f32[4,32,16,128]{3,2,1,0:T(8,128)S(1)} %copy-done), custom_call_target="tpu_custom_call" | custom-call | tf_op jit(solution)/shard_map/gather/pallas_call | solution.py:435
  57.7 0.0 copy-start.3
  57.7 0.7 copy-done.3
  58.4 12.1 %solve.1.potential_ref = f32[16,16,128]{2,1,0:T(8,128)} custom-call(s32[1,3]{1,0:T(1,128)} %start_ref.1, f32[16]{0:T(128)} %constant.4.clone.weight_ref, f32[32,16,128]{2,1,0:T(8,128)} %copy-done.3), custom_call_target="tpu_custom_call" | custom-call | tf_op jit(solution)/shard_map/solve/pallas_call | solution.py:448
  70.5 0.0 copy-start.2
  70.5 0.9 copy-done.2
  71.4 25.1 %scatter.1.terms_ref = f32[4,32,16,128]{3,2,1,0:T(8,128)S(1)} custom-call(s32[1024]{0:T(1024)S(1)} %copy-done.4, f32[16,16,128]{2,1,0:T(8,128)S(1)} %copy-done.2, f32[4,32,16,128]{3,2,1,0:T(8,128)S(1)} %get-tuple-element.8.held_ref), custom_call_target="tpu_custom_call" | custom-call | tf_op jit(solution)/shard_map/scatter/pallas_call | solution.py:462
  96.5 0.0 copy-start.1
  96.5 1.0 copy-done.1
  97.5 9.9 %add.5 = f32[64,64,128]{2,1,0:T(8,128)} custom-call(s32[1024]{0:T(1024)} %reshape.19.meta_ref, f32[4,32,16,128]{3,2,1,0:T(8,128)} %copy-done.1, f32[64,64,128]{2,1,0:T(8,128)} %bitcast.14), custom_call_target="tpu_custom_call" | custom-call | tf_op jit(solution)/shard_map/add/pallas_call | solution.py:475
  (1 shorter events, 0.0 us)
Async XLA Ops:
  18.5 13.7 %copy-start.4 = (s32[1024]{0:T(1024)S(1)}, s32[1024]{0:T(1024)}, u32[]{:S(2)}) copy-start(s32[1024]{0:T(1024)} %reshape.19.meta_ref) | copy-start | bytes 12292
  32.2 1.2 %copy-start = (f32[4,32,16,128]{3,2,1,0:T(8,128)S(1)}, f32[4,32,16,128]{3,2,1,0:T(8,128)}, u32[]{:S(2)}) copy-start(f32[4,32,16,128]{3,2,1,0:T(8,128)} %pack.1.packed_ref) | copy-start | bytes 3145732
  57.7 0.7 copy-start.3
  70.5 0.9 copy-start.2
  96.5 1.0 copy-start.1

commit v2 on v1

v2 whole, which is shorter than its diff:
```python
import functools

import jax
import jax.numpy as jnp
import numpy as np
from jax import lax
from jax.experimental import pallas as pl
from jax.experimental.pallas import tpu as pltpu
from jax.sharding import PartitionSpec as P

ITERS = 16
SCREENING = 0.02
CENTER_EIG = 6.0 + SCREENING
HALF_WIDTH = 6.0

MESH = pl.DeviceIdType.MESH
VMEM = pl.BlockSpec(memory_space=pltpu.VMEM)
SMEM = pl.BlockSpec(memory_space=pltpu.SMEM)
F32 = jnp.float32
I32 = jnp.int32
META = 8
CHUNKS = 4
UNROLL = 4


def chebyshev_weights():
    cheb = np.polynomial.chebyshev
    theta, delta = CENTER_EIG, HALF_WIDTH
    sigma = theta / delta
    potential, residue, update = np.zeros(1), np.ones(1), np.ones(1) / theta
    ratio = 1.0 / sigma
    for _ in range(ITERS):
        potential = cheb.chebadd(potential, update)
        applied = cheb.chebsub(theta * update, 6.0 * cheb.chebmulx(update))
        residue = cheb.chebsub(residue, applied)
        ratio_next = 1.0 / (2.0 * sigma - ratio)
        update = cheb.chebadd(ratio_next * ratio * update, 2.0 * ratio_next / delta * residue)
        ratio = ratio_next
    return [float(c) for c in potential[:ITERS]]


WEIGHTS = chebyshev_weights()


def greet(n_slab, n_orb):
    s, o = lax.axis_index("slab"), lax.axis_index("orb")
    barrier = pltpu.get_barrier_semaphore()
    for d in range(1, n_orb):
        pl.semaphore_signal(barrier, 1, device_id={"orb": lax.rem(o + d, n_orb)}, device_id_type=MESH)

    def signal(d, _):
        pl.semaphore_signal(barrier, 1, device_id={"slab": lax.rem(s + d, n_slab)}, device_id_type=MESH)
        return 0

    lax.fori_loop(1, n_slab, signal, 0)
    pl.semaphore_wait(barrier, n_orb - 1 + n_slab - 1)


def remote(src, dst, send, recv, device):
    return pltpu.make_async_remote_copy(
        src_ref=src, dst_ref=dst, send_sem=send, recv_sem=recv, device_id=device, device_id_type=MESH
    )


def lanes_and_rows():
    lane = lax.broadcasted_iota(I32, (8, 128), 1)
    row = lax.broadcasted_iota(I32, (8, 128), 0)
    return lane, row


def inside_y(j, by, lane, row):
    y = 8 * j + 2 * (row >> 1) + (lane >> 6)
    return ((y - by) & 63) < 32


def pair_of(meta_ref, p, n_orb):
    slab, base = lax.div(p, n_orb), META * lax.rem(p, n_orb)
    return [meta_ref[slab, 0, base + k] for k in range(5)]


def loop(low, high, step):
    def run(n, carry):
        step(n)
        return carry

    lax.fori_loop(low, high, run, 0)


def unrolled(low, high, step):
    def run(n, carry):
        step(n)
        return carry

    lax.fori_loop(low, high, run, 0, unroll=UNROLL)


def share(n_slab, n_orb, pair_ref, start_ref, row, trio, joined, meta_v, meta_s, own_sem, send_o, recv_o, send_s, recv_s):
    s, o = lax.axis_index("slab"), lax.axis_index("orb")
    lane = lax.broadcasted_iota(I32, (1, 128), 1) - META * o
    values = [pair_ref[0, 0], pair_ref[0, 1], start_ref[0, 0], start_ref[0, 1], start_ref[0, 2]]
    line = jnp.zeros((1, 128), I32)
    for k, value in enumerate(values):
        line = jnp.where(lane == k, value, line)
    row[...] = line
    trio[o] = line
    greet(n_slab, n_orb)
    copies = [
        remote(row, trio.at[o], send_o.at[d - 1], recv_o.at[d - 1], {"orb": lax.rem(o + d, n_orb)})
        for d in range(1, n_orb)
    ]
    for copy in copies:
        copy.start()
    for copy in copies:
        copy.wait()
    total = trio[0]
    for k in range(1, n_orb):
        total = total + trio[k]
    joined[...] = total
    meta_v[s] = total

    def to(d):
        return remote(joined, meta_v.at[s], send_s.at[d - 1], recv_s.at[d - 1], {"slab": lax.rem(s + d, n_slab)})

    loop(1, n_slab, lambda d: to(d).start())
    loop(1, n_slab, lambda d: to(d).wait())
    local = pltpu.make_async_copy(meta_v, meta_s, own_sem)
    local.start()
    local.wait()


def pack_one(n_orb, orb_dev, meta, orb, packed, dest, q):
    o = lax.axis_index("orb")
    lane, row = lanes_and_rows()
    zz = lane & 63
    i, j, _, by, bz = pair_of(meta, q * n_orb + dest, n_orb)
    hold_i, hold_j = lax.div(i, orb_dev) == o, lax.div(j, orb_dev) == o
    li, lj = lax.rem(i, orb_dev), lax.rem(j, orb_dev)
    whole = []
    for k in range(8):
        a = jnp.where(hold_i, orb[li, 8 * k : 8 * k + 8, :], 1.0)
        b = jnp.where(hold_j, orb[lj, 8 * k : 8 * k + 8, :], 1.0)
        whole.append(a * b)
    folded = []
    for k in range(4):
        v = jnp.where(inside_y(k, by, lane, row), whole[k], whole[k + 4])
        b = bz if k < 2 else (bz + 32) & 63
        folded.append(
            jnp.where(zz + b < 64, pltpu.roll(v, (128 - b) & 127, 1), pltpu.roll(v, (64 - b) & 127, 1))
        )
    for k in range(2):
        packed[dest, q, 8 * k : 8 * k + 8, :] = jnp.where(zz < 32, folded[k], folded[k + 2])


class Ring:
    def __init__(self, n_slab, n_orb, source, target, relay, near_sem, first_sem, last_sem):
        self.o, self.n_orb = lax.axis_index("orb"), n_orb
        self.size, self.source, self.target, self.relay = n_slab // CHUNKS, source, target, relay
        self.near_sem, self.first_sem, self.last_sem = near_sem, first_sem, last_sem

    def plane(self, d):
        return lax.rem(self.o + d, self.n_orb)

    def rows(self, c):
        return pl.ds(c * self.size, self.size)

    def near(self, d, c):
        n = (0 if d == 1 else 1) * CHUNKS + c
        return remote(
            self.source.at[self.plane(d), self.rows(c)], self.target.at[self.o, self.rows(c)],
            self.near_sem.at[0, n], self.near_sem.at[1, n], {"orb": self.plane(d)},
        )

    def first(self, c):
        way = 1 if c < CHUNKS // 2 else self.n_orb - 1
        return remote(
            self.source.at[self.plane(2), self.rows(c)], self.relay.at[c],
            self.first_sem.at[0, c], self.first_sem.at[1, c], {"orb": self.plane(way)},
        )

    def last(self, c):
        way = 1 if c < CHUNKS // 2 else self.n_orb - 1
        return remote(
            self.relay.at[c], self.target.at[self.plane(self.n_orb - way), self.rows(c)],
            self.last_sem.at[0, c], self.last_sem.at[1, c], {"orb": self.plane(way)},
        )

    def pass_on(self, c):
        self.first(c).wait_recv()
        self.last(c).start()

    def arrived(self, c):
        self.near(1, c).wait_recv()
        self.near(self.n_orb - 1, c).wait_recv()
        self.last(c).wait_recv()

    def drain(self):
        for c in range(CHUNKS):
            self.near(1, c).wait_send()
            self.near(self.n_orb - 1, c).wait_send()
            self.first(c).wait_send()
            self.last(c).wait_send()


def solve(start_ref, weight_ref, box, out, rows_a, rows_b, source, ping, pong):
    bx, by = start_ref[0, 0], start_ref[0, 1]
    by32 = by & 31
    lane, row = lanes_and_rows()
    zz = lane & 63
    in_z = (zz >= 16) & (zz < 48)

    def place(xm):
        x0, x1 = (bx + xm - 8) & 63, (bx + xm + 16) & 63
        v0 = jnp.where(xm >= 8, box[x0 >> 1, pl.ds(x0 & 1, 8, 2), :], 0.0)
        v1 = jnp.where(xm < 16, box[x1 >> 1, pl.ds(x1 & 1, 8, 2), :], 0.0)
        for h in range(2):
            for q in range(2):
                a = pltpu.roll(v0, (16 - 64 * h - 32 * q) % 128, 1)
                b = pltpu.roll(v1, (80 - 64 * h - 32 * q) % 128, 1)
                v = jnp.where(in_z, jnp.where(lane < 64, a, b), 0.0)
                for dup in range(4):
                    rows_a[xm, pl.ds(32 * dup + 16 * q + h, 8, 2), :] = v

    unrolled(0, 24, place)

    first = weight_ref[ITERS - 1]

    def fill(xm):
        for k in range(6):
            u = 6 * row + k - 8
            v = rows_a[xm, pl.ds(by32 + 24 + k, 8, 6), :]
            v = jnp.where((u >= 0) & (u < 32), v, 0.0)
            source[xm, k] = v
            ping[xm + 1, k] = first * v
            pong[xm + 1, k] = jnp.zeros((8, 128), F32)

    unrolled(0, 24, fill)

    def close(ref):
        for k in range(6):
            ref[0, k] = pltpu.roll(ref[24, k], 64, 1)
            ref[25, k] = pltpu.roll(ref[1, k], 64, 1)

    def neighbours(ref, x):
        at = [ref[x, k] for k in range(6)]
        sums = []
        for k in range(6):
            below = at[k - 1] if k > 0 else pltpu.roll(at[5], 1, 0)
            above = at[k + 1] if k < 5 else pltpu.roll(at[0], 7, 0)
            sums.append(
                (ref[x - 1, k] + ref[x + 1, k])
                + (below + above)
                + (pltpu.roll(at[k], 1, 1) + pltpu.roll(at[k], 127, 1))
            )
        return sums

    close(ping)

    def step(now, older, index):
        weight = weight_ref[index]
        for xm in range(24):
            sums = neighbours(now, xm + 1)
            for k in range(6):
                older[xm + 1, k] = weight * source[xm, k] + (sums[k] * (1.0 / 3.0) - older[xm + 1, k])
        close(older)

    def two(n):
        step(ping, pong, ITERS - 2 - 2 * n)
        step(pong, ping, ITERS - 3 - 2 * n)

    loop(0, (ITERS - 2) // 2, two)
    weight = weight_ref[0]
    for xm in range(24):
        sums = neighbours(ping, xm + 1)
        for k in range(6):
            rows_b[xm, pl.ds(k, 8, 6), :] = weight * source[xm, k] + (sums[k] * (1.0 / 6.0) - pong[xm + 1, k])

    def twice(xm):
        for m in range(4):
            v = rows_b[xm, 8 + 8 * m : 16 + 8 * m, :]
            rows_a[xm, 8 * m : 8 * m + 8, :] = v
            rows_a[xm, 32 + 8 * m : 40 + 8 * m, :] = v

    unrolled(0, 24, twice)

    def give(x2):
        for plane in range(2):
            ux = (2 * x2 + plane - bx) & 31
            half = (ux >= 16).astype(I32)
            xm = ux + 8 - 24 * half
            pieces = []
            for h in range(2):
                for q in range(2):
                    v = rows_a[xm, pl.ds(32 - by32 + 16 * q + h, 8, 2), :]
                    pieces.append(pltpu.roll(v, (64 * h + 32 * q - 16 + 128 - 64 * half) & 127, 1))
            v = jnp.where(
                lane < 64,
                jnp.where(zz < 32, pieces[0], pieces[1]),
                jnp.where(zz < 32, pieces[2], pieces[3]),
            )
            out[x2, pl.ds(plane, 8, 2), :] = v

    unrolled(0, 16, give)


def main_kernel(
    n_slab, n_orb, orb_dev, pair_ref, start_ref, weight_ref, orb_hbm, terms, meta_v,
    row, trio, joined, meta_s, orb, packed, held, relay, density, box, rows_a, rows_b, source, ping, pong,
    potential, mine, outgoing, relay_back,
    own_sem, load_sem, send_o, recv_o, send_m, recv_m, near_a, first_a, last_a, near_b, first_b, last_b,
    send_d, recv_d, send_p, recv_p,
):
    s, o = lax.axis_index("slab"), lax.axis_index("orb")
    half = n_slab // 2
    load = pltpu.make_async_copy(orb_hbm, orb, load_sem)
    load.start()
    share(n_slab, n_orb, pair_ref, start_ref, row, trio, joined, meta_v, meta_s, own_sem, send_o, recv_o, send_m, recv_m)
    load.wait()

    ring = Ring(n_slab, n_orb, packed, held, relay, near_a, first_a, last_a)
    size = ring.size

    def pack(d, c):
        dest = ring.plane(d)
        into = held if d == 0 else packed
        unrolled(c * size, (c + 1) * size, lambda q: pack_one(n_orb, orb_dev, meta_s, orb, into, dest, q))

    for c in (0, 2, 1, 3):
        pack(2, c)
        ring.first(c).start()
    for c in range(CHUNKS):
        for d in (1, n_orb - 1):
            pack(d, c)
            ring.near(d, c).start()
    for c in (0, 2, 1, 3):
        ring.pass_on(c)
    for c in range(CHUNKS):
        pack(0, c)

    def holders(q):
        i, j, _, _, _ = pair_of(meta_s, q * n_orb + o, n_orb)
        return lax.div(i, orb_dev), lax.div(j, orb_dev)

    def to_owner(q):
        return remote(density.at[q], box.at[s], send_d.at[q], recv_d.at[s], {"slab": q})

    def from_slab(q):
        return remote(density.at[q], box.at[q], send_d.at[q], recv_d.at[q], {"slab": q})

    def pick(q, plane):
        value = held[0, q]
        for k in range(1, n_orb):
            value = jnp.where(plane == k, held[k, q], value)
        return value

    def form(q):
        oi, oj = holders(q)
        left, right = pick(q, oi), pick(q, oj)
        density[q] = jnp.where(oi == oj, left, left * right)

    def send_density(q):
        @pl.when(q != s)
        def _():
            to_owner(q).start()

    for c in range(CHUNKS):
        ring.arrived(c)
        unrolled(c * size, (c + 1) * size, form)
        loop(c * size, (c + 1) * size, send_density)
    box[s] = density[s]
    loop(1, n_slab, lambda d: from_slab(lax.rem(s + d, n_slab)).wait_recv())

    solve(start_ref, weight_ref, box, potential, rows_a, rows_b, source, ping, pong)

    def to_slab(q):
        return remote(potential.at[lax.rem(q, half)], mine.at[s], send_p.at[q], recv_p.at[s], {"slab": q})

    def from_owner(q):
        return remote(potential.at[lax.rem(q, half)], mine.at[q], send_p.at[q], recv_p.at[q], {"slab": q})

    loop(1, n_slab, lambda d: to_slab(lax.rem(s + d, n_slab)).start())
    mine[s] = potential[lax.rem(s, half)]
    back = Ring(n_slab, n_orb, outgoing, terms, relay_back, near_b, first_b, last_b)

    def wait_mine(q):
        @pl.when(q != s)
        def _():
            from_owner(q).wait_recv()

    def term(d, q):
        dest = back.plane(d)
        oi, oj = holders(q)
        left, right = held[oi, q], held[oj, q]
        factor = jnp.where(oi == oj, 1.0, jnp.where(oi == dest, -right, -left))
        into = terms if d == 0 else outgoing
        into[dest, q] = mine[q] * factor

    for c in (0, 2, 1, 3):
        loop(c * size, (c + 1) * size, wait_mine)
        unrolled(c * size, (c + 1) * size, lambda q: term(2, q))
        back.first(c).start()
    for c in range(CHUNKS):
        for d in (1, n_orb - 1):
            unrolled(c * size, (c + 1) * size, lambda q: term(d, q))
            back.near(d, c).start()
    for c in (0, 2, 1, 3):
        back.pass_on(c)
    unrolled(0, n_slab, lambda q: term(0, q))
    for c in range(CHUNKS):
        back.arrived(c)
    ring.drain()
    back.drain()

    def drain(d):
        q = lax.rem(s + d, n_slab)
        to_owner(q).wait_send()
        to_slab(q).wait_send()

    loop(1, n_slab, drain)


def add_kernel(n_pairs, n_orb, orb_dev, meta_ref, terms_ref, orb_hbm, out_ref, orb_ref, load_sem):
    s, o = lax.axis_index("slab"), lax.axis_index("orb")
    load = pltpu.make_async_copy(orb_hbm, orb_ref, load_sem)
    load.start()
    lane, row = lanes_and_rows()
    z = lane & 63
    x = 2 * s + (row & 1)

    def clear(n):
        out_ref[n] = jnp.zeros(out_ref.shape[1:], F32)

    loop(0, orb_dev, clear)
    load.wait()

    def one(p):
        i, j, bx, by, bz = pair_of(meta_ref, p, n_orb)
        hold_i, hold_j = lax.div(i, orb_dev) == o, lax.div(j, orb_dev) == o
        li, lj = lax.rem(i, orb_dev), lax.rem(j, orb_dev)

        def unfolded():
            in_xz = (((x - bx) & 63) < 32) & (((z - bz) & 63) < 32)
            wide = []
            for k in range(4):
                v = terms_ref[lax.rem(p, n_orb), lax.div(p, n_orb), 8 * (k % 2) : 8 * (k % 2) + 8, :]
                b = bz if k < 2 else (bz + 32) & 63
                v = jnp.where(z >= b, pltpu.roll(v, b, 1), pltpu.roll(v, (b + 64) & 127, 1))
                wide.append(jnp.where(in_xz, v, 0.0))
            keep = [inside_y(k, by, lane, row) for k in range(4)]
            return [jnp.where(keep[k], wide[k], 0.0) for k in range(4)] + [
                jnp.where(keep[k], 0.0, wide[k]) for k in range(4)
            ]

        both = hold_i & hold_j

        @pl.when(both)
        def _():
            values = unfolded()
            for k in range(8):
                rows = slice(8 * k, 8 * k + 8)
                out_ref[li, rows, :] = out_ref[li, rows, :] - values[k] * orb_ref[lj, rows, :]
                out_ref[lj, rows, :] = out_ref[lj, rows, :] - values[k] * orb_ref[li, rows, :]

        @pl.when((hold_i | hold_j) & jnp.logical_not(both))
        def _():
            at = jnp.where(hold_i, li, lj)
            values = unfolded()
            for k in range(8):
                rows = slice(8 * k, 8 * k + 8)
                out_ref[at, rows, :] = out_ref[at, rows, :] + values[k]

    loop(0, n_pairs, one)


def body(orbitals, pair_list, box_start):
    n_slab, n_orb = lax.axis_size("slab"), lax.axis_size("orb")
    orb_dev, planes, cells = orbitals.shape
    n_pairs = n_slab * n_orb
    slot = (16, 128)
    slots = (n_orb, n_slab) + slot
    rows = orbitals.reshape(orb_dev, planes, cells // 128, 128).transpose(0, 2, 1, 3)
    rows = rows.reshape(orb_dev, planes * cells // 128, 128)
    weights = jnp.asarray(np.asarray(WEIGHTS, np.float32))
    relay = pltpu.VMEM((CHUNKS, n_slab // CHUNKS) + slot, F32)
    dma = pltpu.SemaphoreType.DMA
    ring_sems = [dma((2, 2 * CHUNKS)), dma((2, CHUNKS)), dma((2, CHUNKS))]
    terms, meta = pl.pallas_call(
        functools.partial(main_kernel, n_slab, n_orb, orb_dev),
        out_shape=[jax.ShapeDtypeStruct(slots, F32), jax.ShapeDtypeStruct((n_slab, 1, 128), I32)],
        in_specs=[SMEM, SMEM, SMEM, pl.BlockSpec(memory_space=pl.ANY)],
        out_specs=[VMEM, VMEM],
        scratch_shapes=[
            pltpu.VMEM((1, 128), I32),
            pltpu.VMEM((n_orb, 1, 128), I32),
            pltpu.VMEM((1, 128), I32),
            pltpu.SMEM((n_slab, 1, 128), I32),
            pltpu.VMEM(rows.shape, F32),
            pltpu.VMEM(slots, F32),
            pltpu.VMEM(slots, F32),
            relay,
            pltpu.VMEM((n_slab,) + slot, F32),
            pltpu.VMEM((n_slab,) + slot, F32),
            pltpu.VMEM((24, 128, 128), F32),
            pltpu.VMEM((24, 48, 128), F32),
            pltpu.VMEM((24, 6, 8, 128), F32),
            pltpu.VMEM((26, 6, 8, 128), F32),
            pltpu.VMEM((26, 6, 8, 128), F32),
            pltpu.VMEM((n_slab // 2,) + slot, F32),
            pltpu.VMEM((n_slab,) + slot, F32),
            pltpu.VMEM(slots, F32),
            relay,
            dma,
            dma,
            dma((n_orb - 1,)),
            dma((n_orb - 1,)),
            dma((n_slab - 1,)),
            dma((n_slab - 1,)),
        ]
        + ring_sems
        + ring_sems
        + [dma((n_slab,))] * 4,
        compiler_params=pltpu.CompilerParams(collective_id=0, has_side_effects=True, vmem_limit_bytes=40 << 20),
        name="exchange",
    )(pair_list, box_start, weights, rows)
    action = pl.pallas_call(
        functools.partial(add_kernel, n_pairs, n_orb, orb_dev),
        out_shape=jax.ShapeDtypeStruct(rows.shape, F32),
        in_specs=[SMEM, VMEM, pl.BlockSpec(memory_space=pl.ANY)],
        out_specs=VMEM,
        scratch_shapes=[pltpu.VMEM(rows.shape, F32), dma],
        name="add",
    )(meta, terms, rows)
    action = action.reshape(orb_dev, cells // 128, planes, 128).transpose(0, 2, 1, 3)
    return action.reshape(orb_dev, planes, cells)


def solution(mesh):
    return jax.shard_map(
        body,
        mesh=mesh,
        in_specs=(P("orb", "slab", None), P(("slab", "orb"), None), P(("slab", "orb"), None)),
        out_specs=P("orb", "slab", None),
        check_vma=False,
    )
```

time: 107 us -> 80.6 us (0.75)
  Pallas kernels: 102 us -> 75 us
    pallas_call x5 -> x1, Pallas kernels: 92.2 us -> 64.9 us  [body(): pl.pallas_call(functools.partial(main_kernel, n_slab, n_orb, orb_dev), ou...]
    unnamed x10 -> x12, local copies, waits for them, and re-layouts: 3.8 us -> 5.12 us
where the time goes in v2:
time: 80.6 us; the launch traced here: 80.2 us
  Pallas kernels  75 us (93%)
  local copies, waits for them, and re-layouts  5.12 us (6%)
    pallas_call x1, Pallas kernels, body(): pl.pallas_call(functools.partial(main_kernel, n_slab, n_orb, orb_dev), ou...  64.9 us
    pallas_call x1, Pallas kernels, body(): pl.pallas_call(functools.partial(add_kernel, n_pairs, n_orb, orb_dev), ou...  10.1 us
    unnamed x12, local copies, waits for them, and re-layouts  5.12 us

profile of v2, /device:TPU:1, one launch (start us, length us, event | category | flops | bytes accessed | tf_op | source)
XLA Modules:
  0.0 80.2 jit_solution(8658677653827351804)
XLA Ops:
  0.0 0.0 copy-start
  0.0 1.6 %copy-done = f32[64,2,4096]{2,1,0:T(2,128)S(1)} copy-done((f32[64,2,4096]{2,1,0:T(2,128)S(1)}, f32[64,2,4096]{2,1,0:T(2,128)}, u32[]{:S(2)}) %copy-start) | copy-done | bytes 2097176
  1.6 0.0 copy-start.3
  1.6 0.7 copy-done.3
  2.2 0.0 copy-start.4
  2.2 0.7 copy-done.4
  2.9 0.0 copy-start.5
  2.9 0.7 copy-done.5
  3.6 64.9 %exchange.1 = (f32[4,32,16,128]{3,2,1,0:T(8,128)S(1)}, s32[32,1,128]{2,1,0:T(1,128)S(1)}) custom-call(s32[1,2]{1,0:T(1,128)S(1)} %copy-done.3, s32[1,3]{1,0:T(1,128)S(1)} %copy-done.4, f32[16]{0:T(128)S(1)} %copy-done.5, f32[64,64,128]{2,1,0:T(8,128)S(1)} %bitcast.11), custom_call_target="tpu_custom_call" | custom-call | tf_op jit(solution)/shard_map/exchange/pallas_call | solution.py:486
  68.5 0.0 copy-start.1
  68.5 1.0 %copy-done.1 = f32[4,32,16,128]{3,2,1,0:T(8,128)} copy-done((f32[4,32,16,128]{3,2,1,0:T(8,128)}, f32[4,32,16,128]{3,2,1,0:T(8,128)S(1)}, u32[]{:S(2)}) %copy-start.1) | copy-done | bytes 1048600
  69.5 0.0 copy-start.2
  69.5 0.6 copy-done.2
  70.1 10.1 %add.1 = f32[64,64,128]{2,1,0:T(8,128)} custom-call(s32[32,1,128]{2,1,0:T(1,128)} %copy-done.2, f32[4,32,16,128]{3,2,1,0:T(8,128)} %copy-done.1, f32[64,64,128]{2,1,0:T(8,128)} %bitcast.10), custom_call_target="tpu_custom_call" | custom-call | tf_op jit(solution)/shard_map/add/pallas_call | solution.py:524
Async XLA Ops:
  0.0 1.6 %copy-start = (f32[64,2,4096]{2,1,0:T(2,128)S(1)}, f32[64,2,4096]{2,1,0:T(2,128)}, u32[]{:S(2)}) copy-start(f32[64,2,4096]{2,1,0:T(2,128)} %param.4) | copy-start | bytes 6291460
  1.6 0.7 copy-start.3
  2.2 0.7 copy-start.4
  2.9 0.7 copy-start.5
  68.5 1.0 %copy-start.1 = (f32[4,32,16,128]{3,2,1,0:T(8,128)}, f32[4,32,16,128]{3,2,1,0:T(8,128)S(1)}, u32[]{:S(2)}) copy-start(f32[4,32,16,128]{3,2,1,0:T(8,128)S(1)} %get-tuple-element.8.terms_ref) | copy-start | bytes 3145732
  69.5 0.6 copy-start.2

commit v3 on v2

v3 whole, which is shorter than its diff:
```python
import functools

import jax
import jax.numpy as jnp
import numpy as np
from jax import lax
from jax.experimental import pallas as pl
from jax.experimental.pallas import tpu as pltpu
from jax.sharding import PartitionSpec as P

ITERS = 16
SCREENING = 0.02
CENTER_EIG = 6.0 + SCREENING
HALF_WIDTH = 6.0

MESH = pl.DeviceIdType.MESH
VMEM = pl.BlockSpec(memory_space=pltpu.VMEM)
SMEM = pl.BlockSpec(memory_space=pltpu.SMEM)
F32 = jnp.float32
I32 = jnp.int32
META = 8
CHUNKS = 4
EXCHANGE_VMEM = 50 << 20
UNROLL = 4


def chebyshev_weights():
    cheb = np.polynomial.chebyshev
    theta, delta = CENTER_EIG, HALF_WIDTH
    sigma = theta / delta
    potential, residue, update = np.zeros(1), np.ones(1), np.ones(1) / theta
    ratio = 1.0 / sigma
    for _ in range(ITERS):
        potential = cheb.chebadd(potential, update)
        applied = cheb.chebsub(theta * update, 6.0 * cheb.chebmulx(update))
        residue = cheb.chebsub(residue, applied)
        ratio_next = 1.0 / (2.0 * sigma - ratio)
        update = cheb.chebadd(ratio_next * ratio * update, 2.0 * ratio_next / delta * residue)
        ratio = ratio_next
    return [float(c) for c in potential[:ITERS]]


WEIGHTS = chebyshev_weights()


def greet(n_slab, n_orb):
    s, o = lax.axis_index("slab"), lax.axis_index("orb")
    barrier = pltpu.get_barrier_semaphore()
    for d in range(1, n_orb):
        pl.semaphore_signal(barrier, 1, device_id={"orb": lax.rem(o + d, n_orb)}, device_id_type=MESH)

    def signal(d, _):
        pl.semaphore_signal(barrier, 1, device_id={"slab": lax.rem(s + d, n_slab)}, device_id_type=MESH)
        return 0

    lax.fori_loop(1, n_slab, signal, 0)
    pl.semaphore_wait(barrier, n_orb - 1 + n_slab - 1)


def remote(src, dst, send, recv, device):
    return pltpu.make_async_remote_copy(
        src_ref=src, dst_ref=dst, send_sem=send, recv_sem=recv, device_id=device, device_id_type=MESH
    )


def lanes_and_rows():
    lane = lax.broadcasted_iota(I32, (8, 128), 1)
    row = lax.broadcasted_iota(I32, (8, 128), 0)
    return lane, row


def inside_y(j, by, lane, row):
    y = 8 * j + 2 * (row >> 1) + (lane >> 6)
    return ((y - by) & 63) < 32


def split(index, count):
    if count & (count - 1):
        return lax.div(index, count), lax.rem(index, count)
    return index >> (count.bit_length() - 1), index & (count - 1)


def pair_of(meta_ref, p, n_orb):
    slab, at = split(p, n_orb)
    return [meta_ref[slab, 0, META * at + k] for k in range(5)]


def loop(low, high, step):
    def run(n, carry):
        step(n)
        return carry

    lax.fori_loop(low, high, run, 0)


def unrolled(low, high, step):
    def run(n, carry):
        step(n)
        return carry

    lax.fori_loop(low, high, run, 0, unroll=UNROLL)


def share(n_slab, n_orb, own_ref, row, trio, joined, meta_v, send_o, recv_o, send_m, recv_m):
    s, o = lax.axis_index("slab"), lax.axis_index("orb")
    row[...] = jnp.zeros((1, 128), I32)
    row[:, 0:5] = own_ref[...]
    line = pltpu.roll(jnp.broadcast_to(row[...], (8, 128)), META * o, 1)[0:1, :]
    row[...] = line
    trio[o] = line
    copies = [
        remote(row, trio.at[o], send_o.at[d - 1], recv_o.at[d - 1], {"orb": lax.rem(o + d, n_orb)})
        for d in range(1, n_orb)
    ]
    for copy in copies:
        copy.start()
    for copy in copies:
        copy.wait()
    total = trio[0]
    for k in range(1, n_orb):
        total = total + trio[k]
    joined[...] = total
    meta_v[s] = total

    def to(q):
        return remote(joined, meta_v.at[s], send_m.at[q], recv_m.at[s], {"slab": q})

    def arrived(q):
        @pl.when(q != s)
        def _():
            remote(joined, meta_v.at[q], send_m.at[q], recv_m.at[q], {"slab": q}).wait_recv()

    loop(1, n_slab, lambda d: to(lax.rem(s + d, n_slab)).start())
    return arrived, lambda d: to(lax.rem(s + d, n_slab)).wait_send()


def pack_one(n_orb, orb_dev, meta, orb, packed, dest, q):
    o = lax.axis_index("orb")
    lane, row = lanes_and_rows()
    zz = lane & 63
    i, j, _, by, bz = pair_of(meta, q * n_orb + dest, n_orb)
    (oi, li), (oj, lj) = split(i, orb_dev), split(j, orb_dev)
    hold_i, hold_j = oi == o, oj == o
    whole = []
    for k in range(8):
        a = jnp.where(hold_i, orb[li, 8 * k : 8 * k + 8, :], 1.0)
        b = jnp.where(hold_j, orb[lj, 8 * k : 8 * k + 8, :], 1.0)
        whole.append(a * b)
    folded = []
    for k in range(4):
        v = jnp.where(inside_y(k, by, lane, row), whole[k], whole[k + 4])
        b = bz if k < 2 else (bz + 32) & 63
        folded.append(
            jnp.where(zz + b < 64, pltpu.roll(v, (128 - b) & 127, 1), pltpu.roll(v, (64 - b) & 127, 1))
        )
    for k in range(2):
        packed[dest, q, 8 * k : 8 * k + 8, :] = jnp.where(zz < 32, folded[k], folded[k + 2])


def weight_of(index):
    value = jnp.float32(WEIGHTS[0])
    for k in range(1, ITERS):
        value = jnp.where(index == k, jnp.float32(WEIGHTS[k]), value)
    return value


def solve(bx, by, box, out, rows_a, rows_b, source, ping, pong):
    by32 = by & 31
    lane, row = lanes_and_rows()
    zz = lane & 63
    in_z = (zz >= 16) & (zz < 48)

    def place(xm):
        x0, x1 = (bx + xm - 8) & 63, (bx + xm + 16) & 63
        v0 = jnp.where(xm >= 8, box[x0 >> 1, pl.ds(x0 & 1, 8, 2), :], 0.0)
        v1 = jnp.where(xm < 16, box[x1 >> 1, pl.ds(x1 & 1, 8, 2), :], 0.0)
        for h in range(2):
            for q in range(2):
                a = pltpu.roll(v0, (16 - 64 * h - 32 * q) % 128, 1)
                b = pltpu.roll(v1, (80 - 64 * h - 32 * q) % 128, 1)
                v = jnp.where(in_z, jnp.where(lane < 64, a, b), 0.0)
                for dup in range(4):
                    rows_a[xm, pl.ds(32 * dup + 16 * q + h, 8, 2), :] = v

    unrolled(0, 24, place)

    first = WEIGHTS[ITERS - 1]

    def fill(xm):
        for k in range(6):
            u = 6 * row + k - 8
            v = rows_a[xm, pl.ds(by32 + 24 + k, 8, 6), :]
            v = jnp.where((u >= 0) & (u < 32), v, 0.0)
            source[xm, k] = v
            ping[xm + 1, k] = first * v
            pong[xm + 1, k] = jnp.zeros((8, 128), F32)

    unrolled(0, 24, fill)

    def close(ref):
        for k in range(6):
            ref[0, k] = pltpu.roll(ref[24, k], 64, 1)
            ref[25, k] = pltpu.roll(ref[1, k], 64, 1)

    def neighbours(ref, x):
        at = [ref[x, k] for k in range(6)]
        sums = []
        for k in range(6):
            below = at[k - 1] if k > 0 else pltpu.roll(at[5], 1, 0)
            above = at[k + 1] if k < 5 else pltpu.roll(at[0], 7, 0)
            sums.append(
                (ref[x - 1, k] + ref[x + 1, k])
                + (below + above)
                + (pltpu.roll(at[k], 1, 1) + pltpu.roll(at[k], 127, 1))
            )
        return sums

    close(ping)

    def step(now, older, index):
        weight = weight_of(index)
        for xm in range(24):
            sums = neighbours(now, xm + 1)
            for k in range(6):
                older[xm + 1, k] = weight * source[xm, k] + (sums[k] * (1.0 / 3.0) - older[xm + 1, k])
        close(older)

    def two(n):
        step(ping, pong, ITERS - 2 - 2 * n)
        step(pong, ping, ITERS - 3 - 2 * n)

    loop(0, (ITERS - 2) // 2, two)
    weight = WEIGHTS[0]
    for xm in range(24):
        sums = neighbours(ping, xm + 1)
        for k in range(6):
            rows_b[xm, pl.ds(k, 8, 6), :] = weight * source[xm, k] + (sums[k] * (1.0 / 6.0) - pong[xm + 1, k])

    def twice(xm):
        for m in range(4):
            v = rows_b[xm, 8 + 8 * m : 16 + 8 * m, :]
            rows_a[xm, 8 * m : 8 * m + 8, :] = v
            rows_a[xm, 32 + 8 * m : 40 + 8 * m, :] = v

    unrolled(0, 24, twice)

    def give(x2):
        for plane in range(2):
            ux = (2 * x2 + plane - bx) & 31
            half = (ux >= 16).astype(I32)
            xm = ux + 8 - 24 * half
            pieces = []
            for h in range(2):
                for q in range(2):
                    v = rows_a[xm, pl.ds(32 - by32 + 16 * q + h, 8, 2), :]
                    pieces.append(pltpu.roll(v, (64 * h + 32 * q - 16 + 128 - 64 * half) & 127, 1))
            v = jnp.where(
                lane < 64,
                jnp.where(zz < 32, pieces[0], pieces[1]),
                jnp.where(zz < 32, pieces[2], pieces[3]),
            )
            out[x2, pl.ds(plane, 8, 2), :] = v

    unrolled(0, 16, give)


def main_kernel(
    n_slab, n_orb, orb_dev, own_ref, orb_hbm, terms, meta_hbm, orb,
    row, trio, joined, meta_v, meta_s, packed, held, relay, combined, density, box,
    rows_a, rows_b, source, ping, pong, potential, mine, to_relay, to_plain, to_far, from_dest,
    load_sem, meta_sem, send_o, recv_o, send_m, recv_m, ring_sem, back_sem, send_d, recv_d, send_p, recv_p,
):
    s, o = lax.axis_index("slab"), lax.axis_index("orb")
    half, size = n_slab // 2, n_slab // CHUNKS
    load = pltpu.make_async_copy(orb_hbm, orb, load_sem)
    load.start()
    greet(n_slab, n_orb)
    row_arrived, row_sent = share(
        n_slab, n_orb, own_ref, row, trio, joined, meta_v, send_o, recv_o, send_m, recv_m
    )

    chunks = [(lax.rem(lax.div(s, size) + k, CHUNKS), way) for k, way in ((0, 1), (2, -1), (1, 1), (3, -1))]

    def plane(d):
        return lax.rem(o + d + n_orb, n_orb)

    def rows(c):
        return pl.ds(c * size, size)

    def chunk_loop(c, step):
        unrolled(0, size, lambda n: step(c * size + n, n))

    def ring_copy(kind, sems, source, target, c, d):
        return remote(source, target, sems.at[kind, 0, c], sems.at[kind, 1, c], {"orb": plane(d)})

    def far(c, way):
        return ring_copy(0, ring_sem, packed.at[plane(2), rows(c)], relay.at[c], c, way)

    def through(c, way):
        return ring_copy(1, ring_sem, combined.at[c], held.at[o, rows(c)], c, way)

    def straight(c, way):
        return ring_copy(2, ring_sem, packed.at[plane(-way), rows(c)], held.at[o, rows(c)], c, -way)

    def pack(d, c, into):
        dest = plane(d)
        chunk_loop(c, lambda q, n: pack_one(n_orb, orb_dev, meta_s, orb, into, dest, q))

    def pass_on(c, way):
        far(c, way).wait_recv()

        def step(q, n):
            combined[c, n] = relay[c, n] * packed[plane(way), q]

        chunk_loop(c, step)
        through(c, way).start()

    for at, (c, way) in enumerate(chunks):
        loop(c * size, (c + 1) * size, row_arrived)
        local = pltpu.make_async_copy(meta_v.at[rows(c)], meta_s.at[rows(c)], meta_sem.at[0])
        local.start()
        local.wait()
        if at == 0:
            load.wait()
        pack(2, c, packed)
        far(c, way).start()
        pack(-way, c, packed)
        straight(c, way).start()
        pack(way, c, packed)
        if at > 0:
            pass_on(*chunks[at - 1])
    keep = pltpu.make_async_copy(meta_v, meta_hbm, meta_sem.at[1])
    keep.start()
    pass_on(*chunks[-1])
    for c, _ in chunks:
        pack(0, c, held)

    def to_owner(q):
        return remote(density.at[q], box.at[s], send_d.at[q], recv_d.at[s], {"slab": q})

    def from_slab(q):
        return remote(density.at[q], box.at[q], send_d.at[q], recv_d.at[q], {"slab": q})

    def send_density(q):
        @pl.when(q != s)
        def _():
            to_owner(q).start()

    for c, way in chunks:
        through(c, way).wait_recv()
        straight(c, way).wait_recv()

        def form(q, n):
            density[q] = held[o, q] * (held[plane(1), q] * held[plane(-1), q])

        chunk_loop(c, form)
        loop(c * size, (c + 1) * size, send_density)
    box[s] = density[s]
    loop(1, n_slab, lambda d: from_slab(lax.rem(s + d, n_slab)).wait_recv())

    _, _, bx, by, _ = pair_of(meta_s, s * n_orb + o, n_orb)
    solve(bx, by, box, potential, rows_a, rows_b, source, ping, pong)

    def to_slab(q):
        return remote(potential.at[lax.rem(q, half)], mine.at[s], send_p.at[q], recv_p.at[s], {"slab": q})

    def from_owner(q):
        return remote(potential.at[lax.rem(q, half)], mine.at[q], send_p.at[q], recv_p.at[q], {"slab": q})

    def send_potential(q):
        @pl.when(q != s)
        def _():
            to_slab(q).start()

    def wait_mine(q):
        @pl.when(q != s)
        def _():
            from_owner(q).wait_recv()

    for c, _ in chunks:
        loop(c * size, (c + 1) * size, send_potential)
    mine[s] = potential[lax.rem(s, half)]

    def back_relay(c, way):
        return ring_copy(0, back_sem, to_relay.at[c], from_dest.at[c], c, -way)

    def back_straight(c, way):
        return ring_copy(1, back_sem, to_plain.at[c], terms.at[o, rows(c)], c, way)

    def back_far(c, way):
        return ring_copy(2, back_sem, to_far.at[c], terms.at[plane(way), rows(c)], c, -way)

    def finish(c, way):
        back_relay(c, way).wait_recv()

        def step(q, n):
            value = from_dest[c, n]
            to_far[c, n] = value * packed[plane(way), q]
            terms[plane(way), q] = value * relay[c, n]

        chunk_loop(c, step)
        back_far(c, way).start()

    for at, (c, way) in enumerate(chunks):
        loop(c * size, (c + 1) * size, wait_mine)

        def share_out(q, n):
            own = mine[q] * held[o, q]
            to_relay[c, n] = own * held[plane(way), q]
            to_plain[c, n] = own * held[plane(-way), q]

        chunk_loop(c, share_out)
        back_relay(c, way).start()
        back_straight(c, way).start()
        if at > 0:
            finish(*chunks[at - 1])
    finish(*chunks[-1])
    for c, _ in chunks:

        def own_term(q, n):
            terms[o, q] = mine[q] * (held[plane(1), q] * held[plane(-1), q])

        chunk_loop(c, own_term)
    for c, way in chunks:
        back_straight(c, way).wait_recv()
        back_far(c, way).wait_recv()
    for c, way in chunks:
        for copy in (far, through, straight, back_relay, back_straight, back_far):
            copy(c, way).wait_send()

    def drain(d):
        q = lax.rem(s + d, n_slab)
        row_sent(d)
        to_owner(q).wait_send()
        to_slab(q).wait_send()

    loop(1, n_slab, drain)
    keep.wait()


def add_kernel(n_pairs, n_orb, orb_dev, meta_ref, terms_ref, orb_ref, out_ref):
    s, o = lax.axis_index("slab"), lax.axis_index("orb")
    lane, row = lanes_and_rows()
    z = lane & 63
    x = 2 * s + (row & 1)

    def clear(n):
        out_ref[n] = jnp.zeros(out_ref.shape[1:], F32)

    loop(0, orb_dev, clear)

    def one(p):
        i, j, bx, by, bz = pair_of(meta_ref, p, n_orb)
        (oi, li), (oj, lj) = split(i, orb_dev), split(j, orb_dev)
        hold_i, hold_j = oi == o, oj == o

        owner_slab, owner_orb = split(p, n_orb)

        def unfolded():
            in_xz = (((x - bx) & 63) < 32) & (((z - bz) & 63) < 32)
            wide = []
            for k in range(4):
                v = terms_ref[owner_orb, owner_slab, 8 * (k % 2) : 8 * (k % 2) + 8, :]
                b = bz if k < 2 else (bz + 32) & 63
                v = jnp.where(z >= b, pltpu.roll(v, b, 1), pltpu.roll(v, (b + 64) & 127, 1))
                wide.append(jnp.where(in_xz, v, 0.0))
            keep = [inside_y(k, by, lane, row) for k in range(4)]
            return [jnp.where(keep[k], wide[k], 0.0) for k in range(4)] + [
                jnp.where(keep[k], 0.0, wide[k]) for k in range(4)
            ]

        both = hold_i & hold_j

        @pl.when(both)
        def _():
            values = unfolded()
            for k in range(8):
                rows = slice(8 * k, 8 * k + 8)
                out_ref[li, rows, :] = out_ref[li, rows, :] - values[k] * orb_ref[lj, rows, :]
                out_ref[lj, rows, :] = out_ref[lj, rows, :] - values[k] * orb_ref[li, rows, :]

        @pl.when((hold_i | hold_j) & jnp.logical_not(both))
        def _():
            at = jnp.where(hold_i, li, lj)
            values = unfolded()
            for k in range(8):
                rows = slice(8 * k, 8 * k + 8)
                out_ref[at, rows, :] = out_ref[at, rows, :] - values[k]

    loop(0, n_pairs, one)


def body(orbitals, pair_list, box_start):
    n_slab, n_orb = lax.axis_size("slab"), lax.axis_size("orb")
    orb_dev, planes, cells = orbitals.shape
    n_pairs = n_slab * n_orb
    slot = (16, 128)
    slots = (n_orb, n_slab) + slot
    rows = orbitals.reshape(orb_dev, planes, cells // 128, 128).transpose(0, 2, 1, 3)
    rows = rows.reshape(orb_dev, planes * cells // 128, 128)
    dma = pltpu.SemaphoreType.DMA
    hbm = pl.BlockSpec(memory_space=pltpu.HBM)
    all_slots, chunked = pltpu.VMEM(slots, F32), pltpu.VMEM((CHUNKS, n_slab // CHUNKS) + slot, F32)
    slabs = pltpu.VMEM((n_slab,) + slot, F32)
    own = jnp.concatenate([pair_list, box_start], axis=1)
    terms, meta, orb_near = pl.pallas_call(
        functools.partial(main_kernel, n_slab, n_orb, orb_dev),
        out_shape=[
            jax.ShapeDtypeStruct(slots, F32),
            jax.ShapeDtypeStruct((n_slab, 1, 128), I32),
            jax.ShapeDtypeStruct(rows.shape, F32),
        ],
        in_specs=[VMEM, hbm],
        out_specs=[VMEM, hbm, VMEM],
        scratch_shapes=[
            pltpu.VMEM((1, 128), I32),
            pltpu.VMEM((n_orb, 1, 128), I32),
            pltpu.VMEM((1, 128), I32),
            pltpu.VMEM((n_slab, 1, 128), I32),
            pltpu.SMEM((n_slab, 1, 128), I32),
            all_slots,
            all_slots,
            chunked,
            chunked,
            slabs,
            slabs,
            pltpu.VMEM((24, 128, 128), F32),
            pltpu.VMEM((24, 48, 128), F32),
            pltpu.VMEM((24, 6, 8, 128), F32),
            pltpu.VMEM((26, 6, 8, 128), F32),
            pltpu.VMEM((26, 6, 8, 128), F32),
            pltpu.VMEM((n_slab // 2,) + slot, F32),
            slabs,
            chunked,
            chunked,
            chunked,
            chunked,
            dma,
            dma((2,)),
            dma((n_orb - 1,)),
            dma((n_orb - 1,)),
            dma((n_slab,)),
            dma((n_slab,)),
            dma((3, 2, CHUNKS)),
            dma((3, 2, CHUNKS)),
            dma((n_slab,)),
            dma((n_slab,)),
            dma((n_slab,)),
            dma((n_slab,)),
        ],
        compiler_params=pltpu.CompilerParams(collective_id=0, has_side_effects=True, vmem_limit_bytes=EXCHANGE_VMEM),
        name="exchange",
    )(own, rows)
    action = pl.pallas_call(
        functools.partial(add_kernel, n_pairs, n_orb, orb_dev),
        out_shape=jax.ShapeDtypeStruct(rows.shape, F32),
        in_specs=[SMEM, VMEM, VMEM],
        out_specs=VMEM,
        compiler_params=pltpu.CompilerParams(vmem_limit_bytes=16 << 20),
        name="add",
    )(meta, terms, orb_near)
    action = action.reshape(orb_dev, cells // 128, planes, 128).transpose(0, 2, 1, 3)
    return action.reshape(orb_dev, planes, cells)


def solution(mesh):
    return jax.shard_map(
        body,
        mesh=mesh,
        in_specs=(P("orb", "slab", None), P(("slab", "orb"), None), P(("slab", "orb"), None)),
        out_specs=P("orb", "slab", None),
        check_vma=False,
    )
```

time: 80.6 us -> 69.4 us (0.86)
  Pallas kernels: 75 us -> 68.3 us
  local copies, waits for them, and re-layouts: 5.12 us -> 0 us
    unnamed x12 -> x0, local copies, waits for them, and re-layouts: 5.12 us -> none
    pallas_call x1, Pallas kernels: 64.9 us -> 60 us  [body(): pl.pallas_call(functools.partial(main_kernel, n_slab, n_orb, orb_dev), ou...]
    pallas_call x1, Pallas kernels: 10.1 us -> 8.26 us  [body(): pl.pallas_call(functools.partial(add_kernel, n_pairs, n_orb, orb_dev), ou...]
where the time goes in v3:
time: 69.4 us; the launch traced here: 69 us
  Pallas kernels  68.3 us (98%)
  other arithmetic  0.75 us (1%)
    pallas_call x1, Pallas kernels, body(): pl.pallas_call(functools.partial(main_kernel, n_slab, n_orb, orb_dev), ou...  60 us
    pallas_call x1, Pallas kernels, body(): pl.pallas_call(functools.partial(add_kernel, n_pairs, n_orb, orb_dev), ou...  8.26 us

profile of v3, /device:TPU:1, one launch (start us, length us, event | category | flops | bytes accessed | tf_op | source)
XLA Modules:
  0.0 69.0 jit_solution(9049681073896884202)
XLA Ops:
  0.0 0.7 %pad_add_fusion.own_ref = s32[1,5]{1,0:T(1,128)S(1)} fusion(s32[1,3]{1,0:T(1,128)} %param.5, s32[1,2]{1,0:T(1,128)} %param.4), kind=kLoop, calls=%fused_computation | loop fusion | flops 5 | bytes 40 | tf_op jit(solution)/shard_map/concatenate | solution.py:505
  0.7 60.0 %exchange.1 = (f32[4,32,16,128]{3,2,1,0:T(8,128)S(1)}, s32[32,1,128]{2,1,0:T(1,128)S(1)}, f32[64,64,128]{2,1,0:T(8,128)S(1)}) custom-call(s32[1,5]{1,0:T(1,128)S(1)} %pad_add_fusion.own_ref, f32[64,64,128]{2,1,0:T(8,128)} %bitcast.10), custom_call_target="tpu_custom_call" | custom-call | tf_op jit(solution)/shard_map/exchange/pallas_call | solution.py:506
  60.8 8.3 %add.3 = f32[64,64,128]{2,1,0:T(8,128)} custom-call(s32[32,1,128]{2,1,0:T(1,128)S(1)} %get-tuple-element.8.meta_ref, f32[4,32,16,128]{3,2,1,0:T(8,128)S(1)} %get-tuple-element.9.terms_ref, f32[64,64,128]{2,1,0:T(8,128)S(1)} %get-tuple-element.10.orb_ref), custom_call_target="tpu_custom_call" | custom-call | tf_op jit(solution)/shard_map/add/pallas_call | solution.py:554

commit v4 on v3

--- a/solution.py
+++ b/solution.py
@@ -22,6 +22,7 @@
 CHUNKS = 4
 EXCHANGE_VMEM = 50 << 20
 UNROLL = 4
+TOGETHER = 4
 
 
 def chebyshev_weights():
@@ -324,14 +325,14 @@
             load.wait()
         pack(2, c, packed)
         far(c, way).start()
+    keep = pltpu.make_async_copy(meta_v, meta_hbm, meta_sem.at[1])
+    keep.start()
+    for c, way in chunks:
         pack(-way, c, packed)
         straight(c, way).start()
+    for c, way in chunks:
         pack(way, c, packed)
-        if at > 0:
-            pass_on(*chunks[at - 1])
-    keep = pltpu.make_async_copy(meta_v, meta_hbm, meta_sem.at[1])
-    keep.start()
-    pass_on(*chunks[-1])
+        pass_on(c, way)
     for c, _ in chunks:
         pack(0, c, held)
 
@@ -401,7 +402,7 @@
         chunk_loop(c, step)
         back_far(c, way).start()
 
-    for at, (c, way) in enumerate(chunks):
+    for c, way in chunks:
         loop(c * size, (c + 1) * size, wait_mine)
 
         def share_out(q, n):
@@ -412,9 +413,8 @@
         chunk_loop(c, share_out)
         back_relay(c, way).start()
         back_straight(c, way).start()
-        if at > 0:
-            finish(*chunks[at - 1])
-    finish(*chunks[-1])
+    for c, way in chunks:
+        finish(c, way)
     for c, _ in chunks:
 
         def own_term(q, n):
@@ -438,56 +438,54 @@
     keep.wait()
 
 
-def add_kernel(n_pairs, n_orb, orb_dev, meta_ref, terms_ref, orb_ref, out_ref):
+def add_kernel(n_pairs, n_orb, orb_dev, meta_ref, terms_ref, orb_ref, out_ref, entries):
     s, o = lax.axis_index("slab"), lax.axis_index("orb")
     lane, row = lanes_and_rows()
     z = lane & 63
     x = 2 * s + (row & 1)
-
-    def clear(n):
-        out_ref[n] = jnp.zeros(out_ref.shape[1:], F32)
-
-    loop(0, orb_dev, clear)
-
-    def one(p):
-        i, j, bx, by, bz = pair_of(meta_ref, p, n_orb)
+    clear = out_ref.shape[1] * orb_dev // n_pairs
+
+    def collect(p, count):
+        i, j = pair_of(meta_ref, p, n_orb)[:2]
         (oi, li), (oj, lj) = split(i, orb_dev), split(j, orb_dev)
-        hold_i, hold_j = oi == o, oj == o
-
+        both = (oi == oj).astype(I32) * orb_dev
+        entries[count] = ((both + lj) * orb_dev + li) * n_pairs + p
+        count = count + (oi == o).astype(I32)
+        entries[count] = ((both + li) * orb_dev + lj) * n_pairs + p
+        count = count + (oj == o).astype(I32)
+        at, part = split(p, n_pairs // orb_dev)
+        out_ref[at, pl.ds(pl.multiple_of(part * clear, clear), clear), :] = jnp.zeros((clear, 128), F32)
+        return count
+
+    count = lax.fori_loop(0, n_pairs, collect, 0, unroll=UNROLL)
+    for k in range(TOGETHER):
+        entries[count + k] = 0
+
+    def value_of(index):
+        rest, p = split(entries[index], n_pairs)
+        rest, at = split(rest, orb_dev)
+        both, other = split(rest, orb_dev)
+        _, _, bx, by, bz = pair_of(meta_ref, p, n_orb)
         owner_slab, owner_orb = split(p, n_orb)
-
-        def unfolded():
-            in_xz = (((x - bx) & 63) < 32) & (((z - bz) & 63) < 32)
-            wide = []
-            for k in range(4):
-                v = terms_ref[owner_orb, owner_slab, 8 * (k % 2) : 8 * (k % 2) + 8, :]
-                b = bz if k < 2 else (bz + 32) & 63
-                v = jnp.where(z >= b, pltpu.roll(v, b, 1), pltpu.roll(v, (b + 64) & 127, 1))
-                wide.append(jnp.where(in_xz, v, 0.0))
-            keep = [inside_y(k, by, lane, row) for k in range(4)]
-            return [jnp.where(keep[k], wide[k], 0.0) for k in range(4)] + [
-                jnp.where(keep[k], 0.0, wide[k]) for k in range(4)
-            ]
-
-        both = hold_i & hold_j
-
-        @pl.when(both)
-        def _():
-            values = unfolded()
+        in_xz = (((x - bx) & 63) < 32) & (((z - bz) & 63) < 32) & (index < count)
+        wide = []
+        for k in range(4):
+            v = terms_ref[owner_orb, owner_slab, 8 * (k % 2) : 8 * (k % 2) + 8, :]
+            b = bz if k < 2 else (bz + 32) & 63
+            v = jnp.where(z >= b, pltpu.roll(v, b, 1), pltpu.roll(v, (b + 64) & 127, 1))
+            wide.append(jnp.where(in_xz, v, 0.0))
+        keep = [inside_y(k, by, lane, row) for k in range(4)]
+        values = [jnp.where(keep[k], wide[k], 0.0) for k in range(4)]
+        values += [jnp.where(keep[k], 0.0, wide[k]) for k in range(4)]
+        factors = [jnp.where(both > 0, orb_ref[other, 8 * k : 8 * k + 8, :], 1.0) for k in range(8)]
+        return at, [value * factor for value, factor in zip(values, factors)]
+
+    def several(n):
+        for at, values in [value_of(TOGETHER * n + k) for k in range(TOGETHER)]:
             for k in range(8):
-                rows = slice(8 * k, 8 * k + 8)
-                out_ref[li, rows, :] = out_ref[li, rows, :] - values[k] * orb_ref[lj, rows, :]
-                out_ref[lj, rows, :] = out_ref[lj, rows, :] - values[k] * orb_ref[li, rows, :]
-
-        @pl.when((hold_i | hold_j) & jnp.logical_not(both))
-        def _():
-            at = jnp.where(hold_i, li, lj)
-            values = unfolded()
-            for k in range(8):
-                rows = slice(8 * k, 8 * k + 8)
-                out_ref[at, rows, :] = out_ref[at, rows, :] - values[k]
-
-    loop(0, n_pairs, one)
+                out_ref[at, 8 * k : 8 * k + 8, :] = out_ref[at, 8 * k : 8 * k + 8, :] - values[k]
+
+    loop(0, lax.div(count + TOGETHER - 1, TOGETHER), several)
 
 
 def body(orbitals, pair_list, box_start):
@@ -556,6 +554,7 @@
         out_shape=jax.ShapeDtypeStruct(rows.shape, F32),
         in_specs=[SMEM, VMEM, VMEM],
         out_specs=VMEM,
+        scratch_shapes=[pltpu.SMEM((2 * n_pairs + TOGETHER,), I32)],
         compiler_params=pltpu.CompilerParams(vmem_limit_bytes=16 << 20),
         name="add",
     )(meta, terms, orb_near)

time: 69.4 us -> 64.9 us (0.935)
  Pallas kernels: 68.3 us -> 63.5 us
    pallas_call x1, Pallas kernels: 8.26 us -> 5.72 us  [body(): pl.pallas_call(functools.partial(add_kernel, n_pairs, n_orb, orb_dev), ou...]
    pallas_call x1, Pallas kernels: 60 us -> 57.8 us  [body(): pl.pallas_call(functools.partial(main_kernel, n_slab, n_orb, orb_dev), ou...]
where the time goes in v4:
time: 64.9 us; the launch traced here: 64.3 us
  Pallas kernels  63.5 us (98%)
  other arithmetic  0.75 us (1%)
    pallas_call x1, Pallas kernels, body(): pl.pallas_call(functools.partial(main_kernel, n_slab, n_orb, orb_dev), ou...  57.8 us
    pallas_call x1, Pallas kernels, body(): pl.pallas_call(functools.partial(add_kernel, n_pairs, n_orb, orb_dev), ou...  5.72 us

profile of v4, /device:TPU:1, one launch (start us, length us, event | category | flops | bytes accessed | tf_op | source)
XLA Modules:
  0.0 64.3 jit_solution(15273123268546358415)
XLA Ops:
  0.0 0.7 %pad_add_fusion.own_ref = s32[1,5]{1,0:T(1,128)S(1)} fusion(s32[1,3]{1,0:T(1,128)} %param.5, s32[1,2]{1,0:T(1,128)} %param.4), kind=kLoop, calls=%fused_computation | loop fusion | flops 5 | bytes 40 | tf_op jit(solution)/shard_map/concatenate | solution.py:503
  0.7 57.8 %exchange.1 = (f32[4,32,16,128]{3,2,1,0:T(8,128)S(1)}, s32[32,1,128]{2,1,0:T(1,128)S(1)}, f32[64,64,128]{2,1,0:T(8,128)S(1)}) custom-call(s32[1,5]{1,0:T(1,128)S(1)} %pad_add_fusion.own_ref, f32[64,64,128]{2,1,0:T(8,128)} %bitcast.10), custom_call_target="tpu_custom_call" | custom-call | tf_op jit(solution)/shard_map/exchange/pallas_call | solution.py:504
  58.5 5.7 %add.3 = f32[64,64,128]{2,1,0:T(8,128)} custom-call(s32[32,1,128]{2,1,0:T(1,128)S(1)} %get-tuple-element.8.meta_ref, f32[4,32,16,128]{3,2,1,0:T(8,128)S(1)} %get-tuple-element.9.terms_ref, f32[64,64,128]{2,1,0:T(8,128)S(1)} %get-tuple-element.10.orb_ref), custom_call_target="tpu_custom_call" | custom-call | tf_op jit(solution)/shard_map/add/pallas_call | solution.py:552

commit v5 on v4

--- a/solution.py
+++ b/solution.py
@@ -44,17 +44,33 @@
 WEIGHTS = chebyshev_weights()
 
 
+SIDE = 4
+FAR_FIRST = (2, 1, 3, 0)
+STEPS = ((0, 1), (2, -1), (1, 1), (3, -1))
+
+
+def peers_at(s, dy):
+    y, x = s // (2 * SIDE), (s // 2) % SIDE
+    row = 2 * SIDE * ((y + dy) % SIDE)
+    found = []
+    for dx in FAR_FIRST:
+        chip = row + 2 * ((x + dx) % SIDE)
+        found += [s ^ 1] if dx == dy == 0 else [chip, chip + 1]
+    return found
+
+
+def peers(s):
+    return [q for dy in FAR_FIRST for q in peers_at(s, dy)]
+
+
 def greet(n_slab, n_orb):
     s, o = lax.axis_index("slab"), lax.axis_index("orb")
     barrier = pltpu.get_barrier_semaphore()
+    for q in peers(s):
+        pl.semaphore_signal(barrier, 1, device_id={"slab": q}, device_id_type=MESH)
     for d in range(1, n_orb):
         pl.semaphore_signal(barrier, 1, device_id={"orb": lax.rem(o + d, n_orb)}, device_id_type=MESH)
 
-    def signal(d, _):
-        pl.semaphore_signal(barrier, 1, device_id={"slab": lax.rem(s + d, n_slab)}, device_id_type=MESH)
-        return 0
-
-    lax.fori_loop(1, n_slab, signal, 0)
     pl.semaphore_wait(barrier, n_orb - 1 + n_slab - 1)
 
 
@@ -127,12 +143,11 @@
         return remote(joined, meta_v.at[s], send_m.at[q], recv_m.at[s], {"slab": q})
 
     def arrived(q):
-        @pl.when(q != s)
-        def _():
-            remote(joined, meta_v.at[q], send_m.at[q], recv_m.at[q], {"slab": q}).wait_recv()
-
-    loop(1, n_slab, lambda d: to(lax.rem(s + d, n_slab)).start())
-    return arrived, lambda d: to(lax.rem(s + d, n_slab)).wait_send()
+        remote(joined, meta_v.at[q], send_m.at[q], recv_m.at[q], {"slab": q}).wait_recv()
+
+    for q in peers(s):
+        to(q).start()
+    return arrived, lambda q: to(q).wait_send()
 
 
 def pack_one(n_orb, orb_dev, meta, orb, packed, dest, q):
@@ -280,7 +295,7 @@
         n_slab, n_orb, own_ref, row, trio, joined, meta_v, send_o, recv_o, send_m, recv_m
     )
 
-    chunks = [(lax.rem(lax.div(s, size) + k, CHUNKS), way) for k, way in ((0, 1), (2, -1), (1, 1), (3, -1))]
+    chunks = [(lax.rem(lax.div(s, size) + k, CHUNKS), way) for k, way in STEPS]
 
     def plane(d):
         return lax.rem(o + d + n_orb, n_orb)
@@ -317,7 +332,8 @@
         through(c, way).start()
 
     for at, (c, way) in enumerate(chunks):
-        loop(c * size, (c + 1) * size, row_arrived)
+        for q in peers_at(s, STEPS[at][0]):
+            row_arrived(q)
         local = pltpu.make_async_copy(meta_v.at[rows(c)], meta_s.at[rows(c)], meta_sem.at[0])
         local.start()
         local.wait()
@@ -342,12 +358,7 @@
     def from_slab(q):
         return remote(density.at[q], box.at[q], send_d.at[q], recv_d.at[q], {"slab": q})
 
-    def send_density(q):
-        @pl.when(q != s)
-        def _():
-            to_owner(q).start()
-
-    for c, way in chunks:
+    for at, (c, way) in enumerate(chunks):
         through(c, way).wait_recv()
         straight(c, way).wait_recv()
 
@@ -355,9 +366,11 @@
             density[q] = held[o, q] * (held[plane(1), q] * held[plane(-1), q])
 
         chunk_loop(c, form)
-        loop(c * size, (c + 1) * size, send_density)
+        for q in peers_at(s, STEPS[at][0]):
+            to_owner(q).start()
     box[s] = density[s]
-    loop(1, n_slab, lambda d: from_slab(lax.rem(s + d, n_slab)).wait_recv())
+    for q in peers(s):
+        from_slab(q).wait_recv()
 
     _, _, bx, by, _ = pair_of(meta_s, s * n_orb + o, n_orb)
     solve(bx, by, box, potential, rows_a, rows_b, source, ping, pong)
@@ -368,18 +381,9 @@
     def from_owner(q):
         return remote(potential.at[lax.rem(q, half)], mine.at[q], send_p.at[q], recv_p.at[q], {"slab": q})
 
-    def send_potential(q):
-        @pl.when(q != s)
-        def _():
+    for k, _ in STEPS:
+        for q in peers_at(s, k):
             to_slab(q).start()
-
-    def wait_mine(q):
-        @pl.when(q != s)
-        def _():
-            from_owner(q).wait_recv()
-
-    for c, _ in chunks:
-        loop(c * size, (c + 1) * size, send_potential)
     mine[s] = potential[lax.rem(s, half)]
 
     def back_relay(c, way):
@@ -402,8 +406,9 @@
         chunk_loop(c, step)
         back_far(c, way).start()
 
-    for c, way in chunks:
-        loop(c * size, (c + 1) * size, wait_mine)
+    for at, (c, way) in enumerate(chunks):
+        for q in peers_at(s, STEPS[at][0]):
+            from_owner(q).wait_recv()
 
         def share_out(q, n):
             own = mine[q] * held[o, q]
@@ -428,13 +433,10 @@
         for copy in (far, through, straight, back_relay, back_straight, back_far):
             copy(c, way).wait_send()
 
-    def drain(d):
-        q = lax.rem(s + d, n_slab)
-        row_sent(d)
+    for q in peers(s):
+        row_sent(q)
         to_owner(q).wait_send()
         to_slab(q).wait_send()
-
-    loop(1, n_slab, drain)
     keep.wait()
 
 

time: 64.9 us -> 63.7 us (0.982)
    pallas_call x1, Pallas kernels: 57.8 us -> 56.7 us  [body(): pl.pallas_call(functools.partial(main_kernel, n_slab, n_orb, orb_dev), ou...]
where the time goes in v5:
time: 63.7 us; the launch traced here: 63.6 us
  Pallas kernels  62.9 us (99%)
  other arithmetic  0.75 us (1%)
    pallas_call x1, Pallas kernels, body(): pl.pallas_call(functools.partial(main_kernel, n_slab, n_orb, orb_dev), ou...  56.7 us
    pallas_call x1, Pallas kernels, body(): pl.pallas_call(functools.partial(add_kernel, n_pairs, n_orb, orb_dev), ou...  6.18 us

profile of v5, /device:TPU:1, one launch (start us, length us, event | category | flops | bytes accessed | tf_op | source)
XLA Modules:
  0.0 63.6 jit_solution(1435659436539909860)
XLA Ops:
  0.0 0.7 %pad_add_fusion.own_ref = s32[1,5]{1,0:T(1,128)S(1)} fusion(s32[1,3]{1,0:T(1,128)} %param.5, s32[1,2]{1,0:T(1,128)} %param.4), kind=kLoop, calls=%fused_computation | loop fusion | flops 5 | bytes 40 | tf_op jit(solution)/shard_map/concatenate | solution.py:505
  0.7 56.7 %exchange.1 = (f32[4,32,16,128]{3,2,1,0:T(8,128)S(1)}, s32[32,1,128]{2,1,0:T(1,128)S(1)}, f32[64,64,128]{2,1,0:T(8,128)S(1)}) custom-call(s32[1,5]{1,0:T(1,128)S(1)} %pad_add_fusion.own_ref, f32[64,64,128]{2,1,0:T(8,128)} %bitcast.10), custom_call_target="tpu_custom_call" | custom-call | tf_op jit(solution)/shard_map/exchange/pallas_call | solution.py:506
  57.4 6.2 %add.3 = f32[64,64,128]{2,1,0:T(8,128)} custom-call(s32[32,1,128]{2,1,0:T(1,128)S(1)} %get-tuple-element.8.meta_ref, f32[4,32,16,128]{3,2,1,0:T(8,128)S(1)} %get-tuple-element.9.terms_ref, f32[64,64,128]{2,1,0:T(8,128)S(1)} %get-tuple-element.10.orb_ref), custom_call_target="tpu_custom_call" | custom-call | tf_op jit(solution)/shard_map/add/pallas_call | solution.py:554

commit v6 on v5

--- a/solution.py
+++ b/solution.py
@@ -47,6 +47,7 @@
 SIDE = 4
 FAR_FIRST = (2, 1, 3, 0)
 STEPS = ((0, 1), (2, -1), (1, 1), (3, -1))
+NEAR_LAST = (1, 2, 3, 0)
 
 
 def peers_at(s, dy):
@@ -63,7 +64,7 @@
     return [q for dy in FAR_FIRST for q in peers_at(s, dy)]
 
 
-def greet(n_slab, n_orb):
+def greet(n_slab, n_orb, meanwhile):
     s, o = lax.axis_index("slab"), lax.axis_index("orb")
     barrier = pltpu.get_barrier_semaphore()
     for q in peers(s):
@@ -71,6 +72,7 @@
     for d in range(1, n_orb):
         pl.semaphore_signal(barrier, 1, device_id={"orb": lax.rem(o + d, n_orb)}, device_id_type=MESH)
 
+    meanwhile()
     pl.semaphore_wait(barrier, n_orb - 1 + n_slab - 1)
 
 
@@ -180,25 +182,73 @@
     return value
 
 
-def solve(bx, by, box, out, rows_a, rows_b, source, ping, pong):
+def cosines(index):
+    turn = index & 63
+    turn = jnp.minimum(turn, 64 - turn)
+    value = jnp.full(index.shape, 1.0, F32)
+    for k in range(1, 33):
+        value = jnp.where(turn == k, float(np.cos(2.0 * np.pi * k / 64.0)), value)
+    return value
+
+
+def mode_of(m):
+    wave = jnp.where(m <= 32, m, m - 32)
+    norm = jnp.where((m == 0) | (m == 32), 0.125, 0.125 * float(np.sqrt(2.0)))
+    return wave, jnp.where(m <= 32, 0, 16), norm
+
+
+def modes(to_modes, from_modes, eigen):
+    lane, row = lanes_and_rows()
+    mode, cell, group = lane & 63, lane & 31, lane >> 5
+    wave, quarter, norm = mode_of(mode)
+    eigen[...] = (2.0 / 3.0) * cosines(wave)
+    zero = jnp.zeros((8, 128), F32)
+    for r in range(4):
+        table = norm * cosines(wave * (8 * r + row) - quarter)
+        for half in range(2):
+            part = jnp.where((lane >> 6) == half, table, 0.0)
+            for g in range(4):
+                top = 128 * half + 32 * g + 8 * r
+                for other in range(4):
+                    to_modes[top : top + 8, 128 * other : 128 * other + 128] = part if other == g else zero
+    for r in range(8):
+        wave, quarter, norm = mode_of(8 * r + row)
+        table = norm * cosines(wave * cell - quarter)
+        for g in range(4):
+            part = jnp.where(group == g, table, 0.0)
+            for half in range(2):
+                top = 128 * g + 64 * half + 8 * r
+                for other in range(2):
+                    from_modes[top : top + 8, 128 * other : 128 * other + 128] = part if other == half else zero
+
+
+def exact_dot(a, b):
+    return jnp.dot(a, b, precision=lax.Precision.HIGHEST, preferred_element_type=F32)
+
+
+def solve(bx, by, box, out, rows_a, rows_b, source, ping, pong, to_modes, from_modes, eigen, pairs, wide, halves):
     by32 = by & 31
     lane, row = lanes_and_rows()
-    zz = lane & 63
-    in_z = (zz >= 16) & (zz < 48)
 
     def place(xm):
         x0, x1 = (bx + xm - 8) & 63, (bx + xm + 16) & 63
-        v0 = jnp.where(xm >= 8, box[x0 >> 1, pl.ds(x0 & 1, 8, 2), :], 0.0)
-        v1 = jnp.where(xm < 16, box[x1 >> 1, pl.ds(x1 & 1, 8, 2), :], 0.0)
+        at = pl.ds(pl.multiple_of(8 * xm, 8), 8)
+        pairs[at, 0:128] = jnp.where(xm >= 8, box[x0 >> 1, pl.ds(x0 & 1, 8, 2), :], 0.0)
+        pairs[at, 128:256] = jnp.where(xm < 16, box[x1 >> 1, pl.ds(x1 & 1, 8, 2), :], 0.0)
+
+    unrolled(0, 24, place)
+    wide[...] = exact_dot(pairs[...], to_modes[...])
+
+    def spread(xm):
+        at = pl.ds(pl.multiple_of(8 * xm, 8), 8)
         for h in range(2):
             for q in range(2):
-                a = pltpu.roll(v0, (16 - 64 * h - 32 * q) % 128, 1)
-                b = pltpu.roll(v1, (80 - 64 * h - 32 * q) % 128, 1)
-                v = jnp.where(in_z, jnp.where(lane < 64, a, b), 0.0)
+                g = 2 * h + q
+                v = wide[at, 128 * g : 128 * g + 128]
                 for dup in range(4):
                     rows_a[xm, pl.ds(32 * dup + 16 * q + h, 8, 2), :] = v
 
-    unrolled(0, 24, place)
+    unrolled(0, 24, spread)
 
     first = WEIGHTS[ITERS - 1]
 
@@ -218,27 +268,34 @@
             ref[0, k] = pltpu.roll(ref[24, k], 64, 1)
             ref[25, k] = pltpu.roll(ref[1, k], 64, 1)
 
-    def neighbours(ref, x):
-        at = [ref[x, k] for k in range(6)]
-        sums = []
+    along_z = eigen[...]
+
+    def doubled(ref, x, at, before, after):
+        values = []
         for k in range(6):
             below = at[k - 1] if k > 0 else pltpu.roll(at[5], 1, 0)
             above = at[k + 1] if k < 5 else pltpu.roll(at[0], 7, 0)
-            sums.append(
-                (ref[x - 1, k] + ref[x + 1, k])
-                + (below + above)
-                + (pltpu.roll(at[k], 1, 1) + pltpu.roll(at[k], 127, 1))
-            )
-        return sums
+            values.append(((before[k] + after[k]) + (below + above)) * (1.0 / 3.0) + along_z * at[k])
+        return values
+
+    def sweep(now, finish):
+        column = lambda x: [now[x, k] for k in range(6)]
+        before, at = column(0), column(1)
+        for xm in range(24):
+            after = column(xm + 2)
+            finish(xm, doubled(now, xm + 1, at, before, after))
+            before, at = at, after
 
     close(ping)
 
     def step(now, older, index):
         weight = weight_of(index)
-        for xm in range(24):
-            sums = neighbours(now, xm + 1)
+
+        def finish(xm, values):
             for k in range(6):
-                older[xm + 1, k] = weight * source[xm, k] + (sums[k] * (1.0 / 3.0) - older[xm + 1, k])
+                older[xm + 1, k] = weight * source[xm, k] + (values[k] - older[xm + 1, k])
+
+        sweep(now, finish)
         close(older)
 
     def two(n):
@@ -246,11 +303,12 @@
         step(pong, ping, ITERS - 3 - 2 * n)
 
     loop(0, (ITERS - 2) // 2, two)
-    weight = WEIGHTS[0]
-    for xm in range(24):
-        sums = neighbours(ping, xm + 1)
+
+    def last(xm, values):
         for k in range(6):
-            rows_b[xm, pl.ds(k, 8, 6), :] = weight * source[xm, k] + (sums[k] * (1.0 / 6.0) - pong[xm + 1, k])
+            rows_b[xm, pl.ds(k, 8, 6), :] = WEIGHTS[0] * source[xm, k] + (values[k] * 0.5 - pong[xm + 1, k])
+
+    sweep(ping, last)
 
     def twice(xm):
         for m in range(4):
@@ -260,22 +318,24 @@
 
     unrolled(0, 24, twice)
 
+    def collect(xm):
+        at = pl.ds(pl.multiple_of(8 * xm, 8), 8)
+        for h in range(2):
+            for q in range(2):
+                g = 2 * h + q
+                wide[at, 128 * g : 128 * g + 128] = rows_a[xm, pl.ds(32 - by32 + 16 * q + h, 8, 2), :]
+
+    unrolled(0, 24, collect)
+    both = exact_dot(wide[...], from_modes[...])
+    for half in range(2):
+        halves[:, half] = both[:, 128 * half : 128 * half + 128].reshape(24, 8, 128)
+
     def give(x2):
         for plane in range(2):
             ux = (2 * x2 + plane - bx) & 31
             half = (ux >= 16).astype(I32)
             xm = ux + 8 - 24 * half
-            pieces = []
-            for h in range(2):
-                for q in range(2):
-                    v = rows_a[xm, pl.ds(32 - by32 + 16 * q + h, 8, 2), :]
-                    pieces.append(pltpu.roll(v, (64 * h + 32 * q - 16 + 128 - 64 * half) & 127, 1))
-            v = jnp.where(
-                lane < 64,
-                jnp.where(zz < 32, pieces[0], pieces[1]),
-                jnp.where(zz < 32, pieces[2], pieces[3]),
-            )
-            out[x2, pl.ds(plane, 8, 2), :] = v
+            out[x2, pl.ds(plane, 8, 2), :] = jnp.where(half == 0, halves[xm, 0], halves[xm, 1])
 
     unrolled(0, 16, give)
 
@@ -283,14 +343,14 @@
 def main_kernel(
     n_slab, n_orb, orb_dev, own_ref, orb_hbm, terms, meta_hbm, orb,
     row, trio, joined, meta_v, meta_s, packed, held, relay, combined, density, box,
-    rows_a, rows_b, source, ping, pong, potential, mine, to_relay, to_plain, to_far, from_dest,
+    rows_a, rows_b, source, ping, pong, to_modes, from_modes, eigen, joint, wide, halves, potential, mine, to_relay, to_plain, to_far, from_dest,
     load_sem, meta_sem, send_o, recv_o, send_m, recv_m, ring_sem, back_sem, send_d, recv_d, send_p, recv_p,
 ):
     s, o = lax.axis_index("slab"), lax.axis_index("orb")
     half, size = n_slab // 2, n_slab // CHUNKS
     load = pltpu.make_async_copy(orb_hbm, orb, load_sem)
     load.start()
-    greet(n_slab, n_orb)
+    greet(n_slab, n_orb, lambda: modes(to_modes, from_modes, eigen))
     row_arrived, row_sent = share(
         n_slab, n_orb, own_ref, row, trio, joined, meta_v, send_o, recv_o, send_m, recv_m
     )
@@ -343,10 +403,12 @@
         far(c, way).start()
     keep = pltpu.make_async_copy(meta_v, meta_hbm, meta_sem.at[1])
     keep.start()
-    for c, way in chunks:
+    for at in NEAR_LAST:
+        c, way = chunks[at]
         pack(-way, c, packed)
         straight(c, way).start()
-    for c, way in chunks:
+    for at in NEAR_LAST:
+        c, way = chunks[at]
         pack(way, c, packed)
         pass_on(c, way)
     for c, _ in chunks:
@@ -358,7 +420,8 @@
     def from_slab(q):
         return remote(density.at[q], box.at[q], send_d.at[q], recv_d.at[q], {"slab": q})
 
-    for at, (c, way) in enumerate(chunks):
+    for at in NEAR_LAST:
+        c, way = chunks[at]
         through(c, way).wait_recv()
         straight(c, way).wait_recv()
 
@@ -373,7 +436,7 @@
         from_slab(q).wait_recv()
 
     _, _, bx, by, _ = pair_of(meta_s, s * n_orb + o, n_orb)
-    solve(bx, by, box, potential, rows_a, rows_b, source, ping, pong)
+    solve(bx, by, box, potential, rows_a, rows_b, source, ping, pong, to_modes, from_modes, eigen, joint, wide, halves)
 
     def to_slab(q):
         return remote(potential.at[lax.rem(q, half)], mine.at[s], send_p.at[q], recv_p.at[s], {"slab": q})
@@ -529,6 +592,12 @@
             pltpu.VMEM((24, 6, 8, 128), F32),
             pltpu.VMEM((26, 6, 8, 128), F32),
             pltpu.VMEM((26, 6, 8, 128), F32),
+            pltpu.VMEM((256, 512), F32),
+            pltpu.VMEM((512, 256), F32),
+            pltpu.VMEM((8, 128), F32),
+            pltpu.VMEM((192, 256), F32),
+            pltpu.VMEM((192, 512), F32),
+            pltpu.VMEM((24, 2, 8, 128), F32),
             pltpu.VMEM((n_slab // 2,) + slot, F32),
             slabs,
             chunked,

time: 63.7 us -> 62.1 us (0.975)
  Pallas kernels: 62.9 us -> 61.3 us
    pallas_call x1, Pallas kernels: 56.7 us -> 55 us  [body(): pl.pallas_call(functools.partial(main_kernel, n_slab, n_orb, orb_dev), ou...]
where the time goes in v6:
time: 62.1 us; the launch traced here: 62 us
  Pallas kernels  61.3 us (99%)
  other arithmetic  0.75 us (1%)
    pallas_call x1, Pallas kernels, body(): pl.pallas_call(functools.partial(main_kernel, n_slab, n_orb, orb_dev), ou...  55 us
    pallas_call x1, Pallas kernels, body(): pl.pallas_call(functools.partial(add_kernel, n_pairs, n_orb, orb_dev), ou...  6.3 us

profile of v6, /device:TPU:1, one launch (start us, length us, event | category | flops | bytes accessed | tf_op | source)
XLA Modules:
  0.0 62.0 jit_solution(13593114944595768309)
XLA Ops:
  0.0 0.7 %pad_add_fusion.own_ref = s32[1,5]{1,0:T(1,128)S(1)} fusion(s32[1,3]{1,0:T(1,128)} %param.5, s32[1,2]{1,0:T(1,128)} %param.4), kind=kLoop, calls=%fused_computation | loop fusion | flops 5 | bytes 40 | tf_op jit(solution)/shard_map/concatenate | solution.py:568
  0.7 55.0 %exchange.1 = (f32[4,32,16,128]{3,2,1,0:T(8,128)S(1)}, s32[32,1,128]{2,1,0:T(1,128)S(1)}, f32[64,64,128]{2,1,0:T(8,128)S(1)}) custom-call(s32[1,5]{1,0:T(1,128)S(1)} %pad_add_fusion.own_ref, f32[64,64,128]{2,1,0:T(8,128)} %bitcast.10), custom_call_target="tpu_custom_call" | custom-call | tf_op jit(solution)/shard_map/exchange/pallas_call | solution.py:569
  55.7 6.3 %add.3 = f32[64,64,128]{2,1,0:T(8,128)} custom-call(s32[32,1,128]{2,1,0:T(1,128)S(1)} %get-tuple-element.8.meta_ref, f32[4,32,16,128]{3,2,1,0:T(8,128)S(1)} %get-tuple-element.9.terms_ref, f32[64,64,128]{2,1,0:T(8,128)S(1)} %get-tuple-element.10.orb_ref), custom_call_target="tpu_custom_call" | custom-call | tf_op jit(solution)/shard_map/add/pallas_call | solution.py:623

commit v7 on v6

--- a/solution.py
+++ b/solution.py
@@ -19,10 +19,10 @@
 F32 = jnp.float32
 I32 = jnp.int32
 META = 8
-CHUNKS = 4
+CHUNKS = 8
 EXCHANGE_VMEM = 50 << 20
 UNROLL = 4
-TOGETHER = 4
+TOGETHER = 8
 
 
 def chebyshev_weights():
@@ -46,8 +46,8 @@
 
 SIDE = 4
 FAR_FIRST = (2, 1, 3, 0)
-STEPS = ((0, 1), (2, -1), (1, 1), (3, -1))
-NEAR_LAST = (1, 2, 3, 0)
+STEPS = (0, 2, 1, 3)
+NEAR_LAST = (2, 3, 4, 5, 6, 7, 0, 1)
 
 
 def peers_at(s, dy):
@@ -355,13 +355,23 @@
         n_slab, n_orb, own_ref, row, trio, joined, meta_v, send_o, recv_o, send_m, recv_m
     )
 
-    chunks = [(lax.rem(lax.div(s, size) + k, CHUNKS), way) for k, way in STEPS]
+    chunks = [
+        (2 * ((s // (2 * SIDE) + k) % SIDE) + part, 1 - 2 * part) for k in STEPS for part in range(2)
+    ]
 
     def plane(d):
         return lax.rem(o + d + n_orb, n_orb)
 
     def rows(c):
         return pl.ds(c * size, size)
+
+    def others(at, act):
+        for n in range(size):
+            q = chunks[at][0] * size + n
+            if at >= 2:
+                act(q)
+            else:
+                pl.when(q != s)(functools.partial(act, q))
 
     def chunk_loop(c, step):
         unrolled(0, size, lambda n: step(c * size + n, n))
@@ -392,11 +402,13 @@
         through(c, way).start()
 
     for at, (c, way) in enumerate(chunks):
-        for q in peers_at(s, STEPS[at][0]):
-            row_arrived(q)
-        local = pltpu.make_async_copy(meta_v.at[rows(c)], meta_s.at[rows(c)], meta_sem.at[0])
-        local.start()
-        local.wait()
+        if at % 2 == 0:
+            for q in peers_at(s, STEPS[at // 2]):
+                row_arrived(q)
+            both = pl.ds(c * size, 2 * size)
+            local = pltpu.make_async_copy(meta_v.at[both], meta_s.at[both], meta_sem.at[0])
+            local.start()
+            local.wait()
         if at == 0:
             load.wait()
         pack(2, c, packed)
@@ -429,8 +441,7 @@
             density[q] = held[o, q] * (held[plane(1), q] * held[plane(-1), q])
 
         chunk_loop(c, form)
-        for q in peers_at(s, STEPS[at][0]):
-            to_owner(q).start()
+        others(at, lambda q: to_owner(q).start())
     box[s] = density[s]
     for q in peers(s):
         from_slab(q).wait_recv()
@@ -444,7 +455,7 @@
     def from_owner(q):
         return remote(potential.at[lax.rem(q, half)], mine.at[q], send_p.at[q], recv_p.at[q], {"slab": q})
 
-    for k, _ in STEPS:
+    for k in STEPS:
         for q in peers_at(s, k):
             to_slab(q).start()
     mine[s] = potential[lax.rem(s, half)]
@@ -470,8 +481,7 @@
         back_far(c, way).start()
 
     for at, (c, way) in enumerate(chunks):
-        for q in peers_at(s, STEPS[at][0]):
-            from_owner(q).wait_recv()
+        others(at, lambda q: from_owner(q).wait_recv())
 
         def share_out(q, n):
             own = mine[q] * held[o, q]

time: 62.1 us -> 60.9 us (0.981)
  Pallas kernels: 61.3 us -> 60.2 us
where the time goes in v7:
time: 60.9 us
  Pallas kernels  60.2 us (99%)
  other arithmetic  0.75 us (1%)
    pallas_call x1, Pallas kernels, body(): pl.pallas_call(functools.partial(main_kernel, n_slab, n_orb, orb_dev), ou...  54.4 us
    pallas_call x1, Pallas kernels, body(): pl.pallas_call(functools.partial(add_kernel, n_pairs, n_orb, orb_dev), ou...  5.8 us

profile of v7, /device:TPU:1, one launch (start us, length us, event | category | flops | bytes accessed | tf_op | source)
XLA Modules:
  0.0 60.9 jit_solution(5254763281041370810)
XLA Ops:
  0.0 0.7 %pad_add_fusion.own_ref = s32[1,5]{1,0:T(1,128)S(1)} fusion(s32[1,3]{1,0:T(1,128)} %param.5, s32[1,2]{1,0:T(1,128)} %param.4), kind=kLoop, calls=%fused_computation | loop fusion | flops 5 | bytes 40 | tf_op jit(solution)/shard_map/concatenate | solution.py:578
  0.7 54.4 %exchange.1 = (f32[4,32,16,128]{3,2,1,0:T(8,128)S(1)}, s32[32,1,128]{2,1,0:T(1,128)S(1)}, f32[64,64,128]{2,1,0:T(8,128)S(1)}) custom-call(s32[1,5]{1,0:T(1,128)S(1)} %pad_add_fusion.own_ref, f32[64,64,128]{2,1,0:T(8,128)} %bitcast.10), custom_call_target="tpu_custom_call" | custom-call | tf_op jit(solution)/shard_map/exchange/pallas_call | solution.py:579
  55.1 5.8 %add.3 = f32[64,64,128]{2,1,0:T(8,128)} custom-call(s32[32,1,128]{2,1,0:T(1,128)S(1)} %get-tuple-element.8.meta_ref, f32[4,32,16,128]{3,2,1,0:T(8,128)S(1)} %get-tuple-element.9.terms_ref, f32[64,64,128]{2,1,0:T(8,128)S(1)} %get-tuple-element.10.orb_ref), custom_call_target="tpu_custom_call" | custom-call | tf_op jit(solution)/shard_map/add/pallas_call | solution.py:633

commit v8 on v7

--- a/solution.py
+++ b/solution.py
@@ -46,7 +46,7 @@
 
 SIDE = 4
 FAR_FIRST = (2, 1, 3, 0)
-STEPS = (0, 2, 1, 3)
+STEPS = (0, 1, 3, 2)
 NEAR_LAST = (2, 3, 4, 5, 6, 7, 0, 1)
 
 
@@ -456,7 +456,7 @@
         return remote(potential.at[lax.rem(q, half)], mine.at[q], send_p.at[q], recv_p.at[q], {"slab": q})
 
     for k in STEPS:
-        for q in peers_at(s, k):
+        for q in reversed(peers_at(s, k)):
             to_slab(q).start()
     mine[s] = potential[lax.rem(s, half)]
 

time: 60.9 us -> 60.7 us (level)
  no operation moved by 1% of the time
where the time goes in v8:
time: 60.7 us; the launch traced here: 60.6 us
  Pallas kernels  59.8 us (99%)
  other arithmetic  0.75 us (1%)
    pallas_call x1, Pallas kernels, body(): pl.pallas_call(functools.partial(main_kernel, n_slab, n_orb, orb_dev), ou...  54.2 us
    pallas_call x1, Pallas kernels, body(): pl.pallas_call(functools.partial(add_kernel, n_pairs, n_orb, orb_dev), ou...  5.63 us

profile of v8, /device:TPU:1, one launch (start us, length us, event | category | flops | bytes accessed | tf_op | source)
XLA Modules:
  0.0 60.6 jit_solution(8433041332364169234)
XLA Ops:
  0.0 0.7 %pad_add_fusion.own_ref = s32[1,5]{1,0:T(1,128)S(1)} fusion(s32[1,3]{1,0:T(1,128)} %param.5, s32[1,2]{1,0:T(1,128)} %param.4), kind=kLoop, calls=%fused_computation | loop fusion | flops 5 | bytes 40 | tf_op jit(solution)/shard_map/concatenate | solution.py:578
  0.7 54.2 %exchange.1 = (f32[4,32,16,128]{3,2,1,0:T(8,128)S(1)}, s32[32,1,128]{2,1,0:T(1,128)S(1)}, f32[64,64,128]{2,1,0:T(8,128)S(1)}) custom-call(s32[1,5]{1,0:T(1,128)S(1)} %pad_add_fusion.own_ref, f32[64,64,128]{2,1,0:T(8,128)} %bitcast.10), custom_call_target="tpu_custom_call" | custom-call | tf_op jit(solution)/shard_map/exchange/pallas_call | solution.py:579
  55.0 5.6 %add.3 = f32[64,64,128]{2,1,0:T(8,128)} custom-call(s32[32,1,128]{2,1,0:T(1,128)S(1)} %get-tuple-element.8.meta_ref, f32[4,32,16,128]{3,2,1,0:T(8,128)S(1)} %get-tuple-element.9.terms_ref, f32[64,64,128]{2,1,0:T(8,128)S(1)} %get-tuple-element.10.orb_ref), custom_call_target="tpu_custom_call" | custom-call | tf_op jit(solution)/shard_map/add/pallas_call | solution.py:633
